TPU v7x, 256 devices: a whole 4x4x8 slice. The times are simulated.
256 devices in a mesh: dom: 128 (over z, y, x), tp: 2 (over core).
Axes of the slice: x: 4, y: 4, z: 8, core: 2. Of those that a mesh axis runs over, the one named last changes fastest.
Arguments:
- node_latent: bfloat16 [131072, 128], P('dom'), may hold values from -6 to 6
- edge_latent: bfloat16 [1048576, 128], P(('dom', 'tp')), may hold values from -6 to 6
- edge_sender: int32 [1048576], P(('dom', 'tp')), may hold values from 0 to 1535, as said below
- edge_receiver: int32 [1048576], P(('dom', 'tp')), may hold values from 0 to 1535, as said below
- edge_count: int32 [256], P(('dom', 'tp')), may hold values from 2048 to 4096, as said below
- send_index: int32 [128, 4, 128], P('dom'), may hold values from -1 to 1023, as said below
- edge_in: bfloat16 [3, 384, 128], P(None, None, 'tp'), may hold values from -0.3125 to 0.3125
- edge_out: bfloat16 [3, 128, 128], P(None, 'tp'), may hold values from -0.5 to 0.5
- node_in: bfloat16 [3, 256, 128], P(None, None, 'tp'), may hold values from -0.375 to 0.375
- node_out: bfloat16 [3, 128, 128], P(None, 'tp'), may hold values from -0.5 to 0.5
Outputs:
- node_result: bfloat16 [131072, 128], P('dom')
- edge_result: bfloat16 [1048576, 128], P(('dom', 'tp'))
Inputs may be any that keep to these rules, and one draw needn't show every extreme that they name: `send_index`: entry [p, k, j] is a local node index of partition p sent to partition (p + o_k) mod 128, with o = (1, -1, 2, -2); -1 marks padding, which stands only after the live entries of a block; live entries of a block are distinct; at least half of each block is live and some block is full. `edge_sender`: an index below 1024 is an owned node of the slot's partition; index 1024 + k * 128 + j is slot j of halo block k; never a padding halo slot. `edge_receiver`: as for edge_sender. `edge_count`: some device block is full.
All inputs are finite; a program needn't handle non-finite values.
Results may differ from a plain program's by a relative error of at most 0.013.
Values may be sent and summed in bfloat16 or wider, within the bound.
A program may use at most 64 MiB of HBM per device.

v0:
```python
import jax
import jax.numpy as jnp
from jax import lax
from jax.sharding import PartitionSpec as P

LAYERS = 3


neighbour_offsets = (1, -1, 2, -2)
norm_floor = 0.25


def from_behind(array, axis, by):
    length = lax.axis_size(axis)
    return lax.ppermute(array, axis, [(i, (i + by) % length) for i in range(length)])


def gather_turned(arrays, axis, dims):
    turned = [jnp.moveaxis(a, dim, 0) for a, dim in zip(arrays, dims)]
    both = jnp.concatenate([t.reshape(len(t), -1) for t in turned], axis=1)
    out, at, gathered = (lax.all_gather(both, axis, axis=0, tiled=True), 0, [])
    for t, dim in zip(turned, dims):
        slab = out[:, at : at + t[0].size].reshape(-1, *t.shape[1:])
        gathered.append(jnp.moveaxis(slab, 0, dim))
        at += t[0].size
    return tuple(gathered)


def copy_for_each(array, axis):
    copies = jnp.broadcast_to(array, (lax.axis_size(axis), *array.shape))
    return lax.all_to_all(copies, axis, split_axis=0, concat_axis=0, tiled=True)


def laid_out(pieces, dim):
    dims = list(pieces.shape[1:])
    dims[dim] *= pieces.shape[0]
    return jnp.moveaxis(pieces, 0, dim).reshape(dims)


def gathered_copies(array, axis, dim):
    pieces = copy_for_each(array, axis)
    return laid_out(pieces, dim)


def in_blocks(array, dim, length):
    dims = array.shape
    pieces = array.reshape(*dims[:dim], length, dims[dim] // length, *dims[dim + 1 :])
    return jnp.moveaxis(pieces, dim, 0)


def sum_at_owner(array, axis, dim):
    length = lax.axis_size(axis)
    pieces = lax.all_to_all(in_blocks(array, dim, length), axis, 0, 0, tiled=True)
    return jnp.sum(pieces.astype(jnp.float32), axis=0)


def layer_norm(values):
    centre = jnp.mean(values, axis=-1, keepdims=True)
    centred = values - centre
    spread = jnp.mean(centred * centred, axis=-1, keepdims=True)
    return centred * lax.rsqrt(spread + norm_floor)


def product(first_operand, second_operand):
    return jnp.dot(first_operand, second_operand, preferred_element_type=jnp.float32)


def column_sum(table, values, exact):
    if exact:
        return lax.dot_general(
            table,
            values,
            (((0,), (0,)), ((), ())),
            precision=lax.Precision.HIGHEST,
            preferred_element_type=jnp.float32,
        )
    return lax.dot_general(
        table, values, (((0,), (0,)), ((), ())), preferred_element_type=jnp.float32
    )


def fetch_halo(nodes_now, pick_table):
    feature_width = nodes_now.shape[1]
    picked = (
        product(pick_table, nodes_now)
        .astype(jnp.bfloat16)
        .reshape(len(neighbour_offsets), -1, feature_width)
    )
    blocks = [
        from_behind(picked[neighbour], "dom", offset)
        for neighbour, offset in enumerate(neighbour_offsets)
    ]
    return jnp.concatenate(blocks, axis=0)


def return_sums(returned, pick_float, owned_sums):
    arrived = [
        from_behind(returned[neighbour].astype(jnp.bfloat16), "dom", -offset).astype(jnp.float32)
        for neighbour, offset in enumerate(neighbour_offsets)
    ]
    return owned_sums + column_sum(pick_float, jnp.concatenate(arrived, axis=0), True)


def local(
    node_latent,
    edge_latent,
    edge_sender,
    edge_receiver,
    edge_count,
    send_index,
    edge_in,
    edge_out,
    node_in,
    node_out,
):
    feature_width = node_latent.shape[1]
    node_total = node_latent.shape[0]
    share_rows = node_total // lax.axis_size("tp")
    first_row = lax.axis_index("tp") * share_rows
    edge_rows = edge_latent.shape[0]
    block_rows = min(512, edge_rows)
    block_count = edge_rows // block_rows
    flat_index = send_index[0].reshape(-1)
    halo_total = flat_index.shape[0]
    extended_total = node_total + halo_total
    pick_match = flat_index[:, None] == jnp.arange(node_total, dtype=jnp.int32)[None, :]
    pick_table = pick_match.astype(jnp.bfloat16)
    pick_float = pick_match.astype(jnp.float32)
    live_edges = jnp.arange(edge_rows, dtype=jnp.int32) < edge_count[0]
    sender_blocks = edge_sender.reshape(block_count, block_rows)
    receiver_blocks = edge_receiver.reshape(block_count, block_rows)
    live_blocks = live_edges.reshape(block_count, block_rows)
    extended_columns = jnp.arange(extended_total, dtype=jnp.int32)
    full_in, full_out = gather_turned((edge_in, edge_out), "tp", (2, 1))
    node_first, node_second = (
        gathered_copies(node_in, "tp", 2),
        gathered_copies(node_out, "tp", 1),
    )
    nodes_now = node_latent
    edges_now = edge_latent
    for layer_index in range(LAYERS):
        halo_rows = fetch_halo(nodes_now, pick_table)
        extended = jnp.concatenate([nodes_now, halo_rows], axis=0)
        weight_in = full_in[layer_index]
        weight_out = full_out[layer_index]

        def edge_block(summed, pieces):
            latent, sender_ids, receiver_ids, live_mask = pieces
            sender_table = (sender_ids[:, None] == extended_columns[None, :]).astype(jnp.bfloat16)
            receiver_table = (receiver_ids[:, None] == extended_columns[None, :]).astype(
                jnp.bfloat16
            )
            sender_rows = product(sender_table, extended).astype(jnp.bfloat16)
            receiver_rows = product(receiver_table, extended).astype(jnp.bfloat16)
            linear = product(latent, weight_in[:feature_width])
            linear = linear + product(sender_rows, weight_in[feature_width : 2 * feature_width])
            linear = linear + product(receiver_rows, weight_in[2 * feature_width :])
            edge_hidden = jnp.maximum(linear, 0.0).astype(jnp.bfloat16)
            message = jnp.where(
                live_mask[:, None], layer_norm(product(edge_hidden, weight_out)), 0.0
            ).astype(jnp.bfloat16)
            message = lax.optimization_barrier(message)
            renewed = (latent.astype(jnp.float32) + message.astype(jnp.float32)).astype(
                jnp.bfloat16
            )
            summed = summed + column_sum(receiver_table, message, False)
            return (summed, renewed)

        start_sums = jnp.zeros((extended_total, feature_width), jnp.float32)
        edge_pieces = (
            edges_now.reshape(block_count, block_rows, feature_width),
            sender_blocks,
            receiver_blocks,
            live_blocks,
        )
        summed, renewed_blocks = lax.scan(edge_block, start_sums, edge_pieces)
        edges_now = renewed_blocks.reshape(edge_rows, feature_width)
        returned = summed[node_total:].reshape(len(neighbour_offsets), -1, feature_width)
        owned_sums = return_sums(returned, pick_float, summed[:node_total])
        share_sum = sum_at_owner(owned_sums.astype(jnp.bfloat16), "tp", 0)
        aggregate = share_sum.astype(jnp.bfloat16)
        own_rows = lax.dynamic_slice_in_dim(nodes_now, first_row, share_rows, 0)
        linear_nodes = product(own_rows, node_first[layer_index][:feature_width]) + product(
            aggregate, node_first[layer_index][feature_width:]
        )
        node_hidden = jnp.maximum(linear_nodes, 0.0).astype(jnp.bfloat16)
        update = product(node_hidden, node_second[layer_index])
        renewed = (own_rows.astype(jnp.float32) + layer_norm(update)).astype(jnp.bfloat16)
        nodes_now = lax.all_gather(renewed, "tp", axis=0, tiled=True)
    return (nodes_now, edges_now)


def solution(mesh):
    return jax.shard_map(
        local,
        mesh=mesh,
        in_specs=(
            P("dom", None),
            P(("dom", "tp"), None),
            P(("dom", "tp")),
            P(("dom", "tp")),
            P(("dom", "tp")),
            P("dom", None, None),
            P(None, None, "tp"),
            P(None, "tp", None),
            P(None, None, "tp"),
            P(None, "tp", None),
        ),
        out_specs=(P("dom", None), P(("dom", "tp"), None)),
        check_vma=False,
    )
```

profile of v0, /device:TPU:3, one launch (start us, length us, event | category | flops | bytes accessed | tf_op | source)
XLA Modules:
  0.0 343.9 jit_solution(11437053277433429103)
XLA Ops:
  3.8 1.8 collective-permute-start.2
  5.6 7.7 %collective-permute-start.3 = (bf16[128,128]{1,0:T(8,128)(2,1)S(1)}, bf16[128,128]{1,0:T(8,128)(2,1)S(1)}, u32[]{:S(2)}, u32[]{:S(2)}) collective-permute-start(bf16[128,128]{1,0:T(8,128)(2,1)S(1)} %get-tuple-element.593), channel_id=1, source_target_pairs={{0,252},{2,254},{4,0},{6,2},{8,4},{10,6},{12,8},{14,10},{16,12},{1... | collective-permute-start | bytes 98312 | tf_op jit(solution)/shard_map/ppermute | solution.py:15
  14.1 4.9 %all-to-all-start = ((bf16[2,3,256,64]{2,3,1,0:T(8,128)(2,1)}), bf16[2,3,256,64]{2,3,1,0:T(8,128)(2,1)S(1)}, u32[]{:S(2)}, u32[]{:S(2)}) async-start(bf16[2,3,256,64]{2,3,1,0:T(8,128)(2,1)} %broadcast_in_dim.72), calls=%async_computation | async-start | bytes 393216 | tf_op jit(solution)/shard_map/all_to_all | solution.py:31
  19.8 2.1 all_gather.12
  23.7 3.5 %all-to-all-start.2 = ((bf16[2,3,64,128]{3,2,1,0:T(8,128)(2,1)}), bf16[2,3,64,128]{3,2,1,0:T(8,128)(2,1)S(1)}, u32[]{:S(2)}, u32[]{:S(2)}) async-start(bf16[2,3,64,128]{3,2,1,0:T(8,128)(2,1)} %broadcast_in_dim.73), calls=%async_computation.2 | async-start | bytes 196608 | tf_op jit(solution)/shard_map/all_to_all | solution.py:31
  30.9 64.5 %while.42 = (s32[]{:T(128)}, f32[1536,128]{1,0:T(8,128)S(1)}, bf16[8,512,128]{2,1,0:T(8,128)(2,1)S(1)}, s32[8,512]{1,0:T(8,128)S(1)}, pred[8,512]{1,0:T(8,128)(4...) while((s32[]{:T(128)}, f32[1536,128]{1,0:T(8,128)S(1)}, ...), condition=%wide.region_3.4_spmd.clone.clone, body=%wide.region_0.3_spmd.clone.clone.sunk | while | flops 675021312 | bytes 5933195 | solution.py:176
  33.8 1.8 fusion.231
  95.4 6.8 %collective-permute-start.4 = (bf16[128,128]{1,0:T(8,128)(2,1)S(1)}, bf16[128,128]{1,0:T(8,128)(2,1)S(1)}, u32[]{:S(2)}, u32[]{:S(2)}) collective-permute-start(bf16[128,128]{1,0:T(8,128)(2,1)S(1)} %get-tuple-element.572), channel_id=1, source_target_pairs={{0,254},{2,0},{4,2},{6,4},{8,6},{10,8},{12,10},{14,12},{16,14},{18... | collective-permute-start | bytes 98312 | tf_op jit(solution)/shard_map/ppermute | solution.py:15
  102.2 6.1 %collective-permute-start.6 = (bf16[128,128]{1,0:T(8,128)(2,1)S(1)}, bf16[128,128]{1,0:T(8,128)(2,1)S(1)}, u32[]{:S(2)}, u32[]{:S(2)}) collective-permute-start(bf16[128,128]{1,0:T(8,128)(2,1)S(1)} %get-tuple-element.574), channel_id=1, source_target_pairs={{0,252},{2,254},{4,0},{6,2},{8,4},{10,6},{12,8},{14,10},{16,12},{1... | collective-permute-start | bytes 98312 | tf_op jit(solution)/shard_map/ppermute | solution.py:15
  109.4 7.4 %collective-permute-done.7 = bf16[128,128]{1,0:T(8,128)(2,1)S(1)} collective-permute-done((bf16[128,128]{1,0:T(8,128)(2,1)S(1)}, bf16[128,128]{1,0:T(8,128)(2,1)S(1)}, u32[]{:S(2)}, u32[]{:S(2)}) %collective-permute-start.7) | collective-permute-done | bytes 32800 | tf_op jit(solution)/shard_map/ppermute | solution.py:15
  117.6 5.3 %all_to_all.25 = bf16[2,512,128]{2,1,0:T(8,128)(2,1)S(1)} all-to-all(bf16[2,512,128]{2,1,0:T(8,128)(2,1)S(1)} %bitcast.176), channel_id=1, replica_groups=mesh['dom'=128,'tp'=2] {'tp'}, dimensions={0} | all-to-all | bytes 524288 | tf_op jit(solution)/shard_map/all_to_all | solution.py:53
  123.5 2.0 all_gather.13
  127.8 7.2 %collective-permute-start.11 = (bf16[128,128]{0,1:T(8,128)(2,1)S(1)}, bf16[128,128]{0,1:T(8,128)(2,1)S(1)}, u32[]{:S(2)}, u32[]{:S(2)}) collective-permute-start(bf16[128,128]{0,1:T(8,128)(2,1)S(1)} %get-tuple-element.589), channel_id=1, source_target_pairs={{0,252},{2,254},{4,0},{6,2},{8,4},{10,6},{12,8},{14,10},{16,12},{1... | collective-permute-start | bytes 98312 | tf_op jit(solution)/shard_map/ppermute | solution.py:15
  137.4 62.8 %while.43 = (s32[]{:T(128)}, f32[1536,128]{1,0:T(8,128)}, bf16[8,512,128]{2,1,0:T(8,128)(2,1)S(1)}, s32[8,512]{1,0:T(8,128)S(1)}, pred[8,512]{1,0:T(8,128)(4,1)S...) while((s32[]{:T(128)}, f32[1536,128]{1,0:T(8,128)}, ...), condition=%wide.region_10.11_spmd.clone.clone, body=%wide.region_7.10_spmd.clone.clone.sunk | while | flops 675021312 | bytes 5932687 | solution.py:176
  139.4 1.8 fusion.245
  142.3 2.0 fusion.247
  146.3 1.8 fusion.245
  149.1 3.1 fusion.247
  154.3 1.8 fusion.245
  157.1 3.1 fusion.247
  162.3 1.8 fusion.245
  165.1 3.1 fusion.247
  170.3 1.8 fusion.245
  173.1 3.1 fusion.247
  178.2 1.8 fusion.245
  181.1 3.1 fusion.247
  186.2 1.8 fusion.245
  189.1 3.1 fusion.247
  194.2 1.8 fusion.245
  197.0 3.1 fusion.247
  203.0 12.6 %collective-permute-start.14 = (bf16[128,128]{1,0:T(8,128)(2,1)S(1)}, bf16[128,128]{1,0:T(8,128)(2,1)S(1)}, u32[]{:S(2)}, u32[]{:S(2)}) collective-permute-start(bf16[128,128]{1,0:T(8,128)(2,1)S(1)} %get-tuple-element.570), channel_id=1, source_target_pairs={{0,252},{2,254},{4,0},{6,2},{8,4},{10,6},{12,8},{14,10},{16,12},{1... | collective-permute-start | bytes 98312 | tf_op jit(solution)/shard_map/ppermute | solution.py:15
  216.6 7.5 %collective-permute-done.15 = bf16[128,128]{1,0:T(8,128)(2,1)S(1)} collective-permute-done((bf16[128,128]{1,0:T(8,128)(2,1)S(1)}, bf16[128,128]{1,0:T(8,128)(2,1)S(1)}, u32[]{:S(2)}, u32[]{:S(2)}) %collective-permute-start.15) | collective-permute-done | bytes 32800 | tf_op jit(solution)/shard_map/ppermute | solution.py:15
  224.9 8.0 %all_to_all.26 = bf16[2,512,128]{2,1,0:T(8,128)(2,1)S(1)} all-to-all(bf16[2,512,128]{2,1,0:T(8,128)(2,1)S(1)} %bitcast.177), channel_id=1, replica_groups=mesh['dom'=128,'tp'=2] {'tp'}, dimensions={0} | all-to-all | bytes 524288 | tf_op jit(solution)/shard_map/all_to_all | solution.py:53
  233.5 2.0 all_gather.14
  237.8 7.2 %collective-permute-start.19 = (bf16[128,128]{0,1:T(8,128)(2,1)S(1)}, bf16[128,128]{0,1:T(8,128)(2,1)S(1)}, u32[]{:S(2)}, u32[]{:S(2)}) collective-permute-start(bf16[128,128]{0,1:T(8,128)(2,1)S(1)} %get-tuple-element.585), channel_id=1, source_target_pairs={{0,252},{2,254},{4,0},{6,2},{8,4},{10,6},{12,8},{14,10},{16,12},{1... | collective-permute-start | bytes 98312 | tf_op jit(solution)/shard_map/ppermute | solution.py:15
  246.7 60.8 %while.44 = (s32[]{:T(128)}, f32[1536,128]{1,0:T(8,128)}, bf16[8,512,128]{2,1,0:T(8,128)(2,1)S(1)}, s32[8,512]{1,0:T(8,128)S(1)}, pred[8,512]{1,0:T(8,128)(4,1)S...) while((s32[]{:T(128)}, f32[1536,128]{1,0:T(8,128)}, ...), condition=%wide.region_17.18_spmd.clone.clone, body=%wide.region_14.17_spmd.clone.clone.sunk | while | flops 675021312 | bytes 9078471 | solution.py:176
  251.3 2.0 fusion.261
  257.8 3.2 fusion.261
  265.6 3.2 fusion.261
  273.3 3.2 fusion.261
  281.1 3.2 fusion.261
  288.8 3.2 fusion.261
  296.5 3.2 fusion.261
  304.3 3.2 fusion.261
  310.6 12.6 %collective-permute-start.22 = (bf16[128,128]{1,0:T(8,128)(2,1)S(1)}, bf16[128,128]{1,0:T(8,128)(2,1)S(1)}, u32[]{:S(2)}, u32[]{:S(2)}) collective-permute-start(bf16[128,128]{1,0:T(8,128)(2,1)S(1)} %get-tuple-element.566), channel_id=1, source_target_pairs={{0,252},{2,254},{4,0},{6,2},{8,4},{10,6},{12,8},{14,10},{16,12},{1... | collective-permute-start | bytes 98312 | tf_op jit(solution)/shard_map/ppermute | solution.py:15
  324.2 7.5 %collective-permute-done.23 = bf16[128,128]{1,0:T(8,128)(2,1)S(1)} collective-permute-done((bf16[128,128]{1,0:T(8,128)(2,1)S(1)}, bf16[128,128]{1,0:T(8,128)(2,1)S(1)}, u32[]{:S(2)}, u32[]{:S(2)}) %collective-permute-start.23) | collective-permute-done | bytes 32800 | tf_op jit(solution)/shard_map/ppermute | solution.py:15
  332.5 7.9 %all_to_all.27 = bf16[2,512,128]{2,1,0:T(8,128)(2,1)S(1)} all-to-all(bf16[2,512,128]{2,1,0:T(8,128)(2,1)S(1)} %bitcast.178), channel_id=1, replica_groups=mesh['dom'=128,'tp'=2] {'tp'}, dimensions={0} | all-to-all | bytes 524288 | tf_op jit(solution)/shard_map/all_to_all | solution.py:53
  341.1 2.0 all_gather.15
  (472 shorter events, 153.5 us)
Async XLA Ops:
  0.6 19.1 %copy-start = (bf16[3,64,128]{2,1,0:T(8,128)(2,1)S(1)}, bf16[3,64,128]{2,1,0:T(8,128)(2,1)}, u32[]{:S(2)}) copy-start(bf16[3,64,128]{2,1,0:T(8,128)(2,1)} %param.23) | copy-start | bytes 147460
  0.6 18.4 %copy-start.4 = (bf16[1024,128]{1,0:T(8,128)(2,1)S(1)}, bf16[1024,128]{1,0:T(8,128)(2,1)}, u32[]{:S(2)}) copy-start(bf16[1024,128]{1,0:T(8,128)(2,1)} %param.16) | copy-start | bytes 786436
  0.7 12.7 %copy-start.13 = (bf16[3,256,64]{1,2,0:T(8,128)(2,1)S(1)}, bf16[3,256,64]{1,2,0:T(8,128)(2,1)}, u32[]{:S(2)}) copy-start(bf16[3,256,64]{1,2,0:T(8,128)(2,1)} %param.24) | copy-start | bytes 294916
  0.7 19.1 %copy-start.7 = (bf16[3,384,64]{1,2,0:T(8,128)(2,1)S(1)}, bf16[3,384,64]{1,2,0:T(8,128)(2,1)}, u32[]{:S(2)}) copy-start(bf16[3,384,64]{1,2,0:T(8,128)(2,1)} %param.22) | copy-start | bytes 442372
  2.2 26.0 %collective-permute-start = (bf16[128,128]{1,0:T(8,128)(2,1)S(1)}, bf16[128,128]{1,0:T(8,128)(2,1)S(1)}, u32[]{:S(2)}, u32[]{:S(2)}) collective-permute-start(bf16[128,128]{1,0:T(8,128)(2,1)S(1)} %get-tuple-element.596), channel_id=1, source_target_pairs={{0,2},{2,4},{4,6},{6,8},{8,10},{10,12},{12,14},{14,16},{16,18},{18... | collective-permute-start | bytes 98312 | tf_op jit(solution)/shard_map/ppermute | solution.py:15
  3.5 25.3 %collective-permute-start.1 = (bf16[128,128]{1,0:T(8,128)(2,1)S(1)}, bf16[128,128]{1,0:T(8,128)(2,1)S(1)}, u32[]{:S(2)}, u32[]{:S(2)}) collective-permute-start(bf16[128,128]{1,0:T(8,128)(2,1)S(1)} %get-tuple-element.595), channel_id=1, source_target_pairs={{0,254},{2,0},{4,2},{6,4},{8,6},{10,8},{12,10},{14,12},{16,14},{18... | collective-permute-start | bytes 98312 | tf_op jit(solution)/shard_map/ppermute | solution.py:15
  3.8 25.7 %collective-permute-start.2 = (bf16[128,128]{1,0:T(8,128)(2,1)S(1)}, bf16[128,128]{1,0:T(8,128)(2,1)S(1)}, u32[]{:S(2)}, u32[]{:S(2)}) collective-permute-start(bf16[128,128]{1,0:T(8,128)(2,1)S(1)} %get-tuple-element.594), channel_id=1, source_target_pairs={{0,4},{2,6},{4,8},{6,10},{8,12},{10,14},{12,16},{14,18},{16,20},{1... | collective-permute-start | bytes 98312 | tf_op jit(solution)/shard_map/ppermute | solution.py:15
  5.6 24.5 %collective-permute-start.3 = (bf16[128,128]{1,0:T(8,128)(2,1)S(1)}, bf16[128,128]{1,0:T(8,128)(2,1)S(1)}, u32[]{:S(2)}, u32[]{:S(2)}) collective-permute-start(bf16[128,128]{1,0:T(8,128)(2,1)S(1)} %get-tuple-element.593), channel_id=1, source_target_pairs={{0,252},{2,254},{4,0},{6,2},{8,4},{10,6},{12,8},{14,10},{16,12},{1... | collective-permute-start | bytes 98312 | tf_op jit(solution)/shard_map/ppermute | solution.py:15
  14.1 9.0 %all-to-all-start = ((bf16[2,3,256,64]{2,3,1,0:T(8,128)(2,1)}), bf16[2,3,256,64]{2,3,1,0:T(8,128)(2,1)S(1)}, u32[]{:S(2)}, u32[]{:S(2)}) async-start(bf16[2,3,256,64]{2,3,1,0:T(8,128)(2,1)} %broadcast_in_dim.72), calls=%async_computation | async-start | bytes 393216 | tf_op jit(solution)/shard_map/all_to_all | solution.py:31
  22.3 5.9 %copy-start.15 = (s32[4096]{0:T(1024)S(1)}, s32[4096]{0:T(1024)}, u32[]{:S(2)}) copy-start(s32[4096]{0:T(1024)} %param.19) | copy-start | bytes 49156
  22.3 5.9 %copy-start.16 = (s32[4096]{0:T(1024)S(1)}, s32[4096]{0:T(1024)}, u32[]{:S(2)}) copy-start(s32[4096]{0:T(1024)} %param.18) | copy-start | bytes 49156
  23.7 84.6 %all-to-all-start.2 = ((bf16[2,3,64,128]{3,2,1,0:T(8,128)(2,1)}), bf16[2,3,64,128]{3,2,1,0:T(8,128)(2,1)S(1)}, u32[]{:S(2)}, u32[]{:S(2)}) async-start(bf16[2,3,64,128]{3,2,1,0:T(8,128)(2,1)} %broadcast_in_dim.73), calls=%async_computation.2 | async-start | bytes 196608 | tf_op jit(solution)/shard_map/all_to_all | solution.py:31
  95.4 21.4 %copy-start.17 = (s32[1,4,128]{2,1,0:T(4,128)S(1)}, s32[1,4,128]{2,1,0:T(4,128)}, u32[]{:S(2)}) copy-start(s32[1,4,128]{2,1,0:T(4,128)} %param.21) | copy-start | bytes 6148
  95.4 13.9 %collective-permute-start.4 = (bf16[128,128]{1,0:T(8,128)(2,1)S(1)}, bf16[128,128]{1,0:T(8,128)(2,1)S(1)}, u32[]{:S(2)}, u32[]{:S(2)}) collective-permute-start(bf16[128,128]{1,0:T(8,128)(2,1)S(1)} %get-tuple-element.572), channel_id=1, source_target_pairs={{0,254},{2,0},{4,2},{6,4},{8,6},{10,8},{12,10},{14,12},{16,14},{18... | collective-permute-start | bytes 98312 | tf_op jit(solution)/shard_map/ppermute | solution.py:15
  102.2 7.1 %collective-permute-start.5 = (bf16[128,128]{1,0:T(8,128)(2,1)S(1)}, bf16[128,128]{1,0:T(8,128)(2,1)S(1)}, u32[]{:S(2)}, u32[]{:S(2)}) collective-permute-start(bf16[128,128]{1,0:T(8,128)(2,1)S(1)} %get-tuple-element.575), channel_id=1, source_target_pairs={{0,2},{2,4},{4,6},{6,8},{8,10},{10,12},{12,14},{14,16},{16,18},{18... | collective-permute-start | bytes 98312 | tf_op jit(solution)/shard_map/ppermute | solution.py:15
  102.2 7.1 %collective-permute-start.6 = (bf16[128,128]{1,0:T(8,128)(2,1)S(1)}, bf16[128,128]{1,0:T(8,128)(2,1)S(1)}, u32[]{:S(2)}, u32[]{:S(2)}) collective-permute-start(bf16[128,128]{1,0:T(8,128)(2,1)S(1)} %get-tuple-element.574), channel_id=1, source_target_pairs={{0,252},{2,254},{4,0},{6,2},{8,4},{10,6},{12,8},{14,10},{16,12},{1... | collective-permute-start | bytes 98312 | tf_op jit(solution)/shard_map/ppermute | solution.py:15
  108.3 8.5 %collective-permute-start.7 = (bf16[128,128]{1,0:T(8,128)(2,1)S(1)}, bf16[128,128]{1,0:T(8,128)(2,1)S(1)}, u32[]{:S(2)}, u32[]{:S(2)}) collective-permute-start(bf16[128,128]{1,0:T(8,128)(2,1)S(1)} %get-tuple-element.573), channel_id=1, source_target_pairs={{0,4},{2,6},{4,8},{6,10},{8,12},{10,14},{12,16},{14,18},{16,20},{1... | collective-permute-start | bytes 98312 | tf_op jit(solution)/shard_map/ppermute | solution.py:15
  126.2 8.8 %collective-permute-start.8 = (bf16[128,128]{0,1:T(8,128)(2,1)S(1)}, bf16[128,128]{0,1:T(8,128)(2,1)S(1)}, u32[]{:S(2)}, u32[]{:S(2)}) collective-permute-start(bf16[128,128]{0,1:T(8,128)(2,1)S(1)} %get-tuple-element.592), channel_id=1, source_target_pairs={{0,2},{2,4},{4,6},{6,8},{8,10},{10,12},{12,14},{14,16},{16,18},{18... | collective-permute-start | bytes 98312 | tf_op jit(solution)/shard_map/ppermute | solution.py:15
  126.3 8.7 %collective-permute-start.9 = (bf16[128,128]{0,1:T(8,128)(2,1)S(1)}, bf16[128,128]{0,1:T(8,128)(2,1)S(1)}, u32[]{:S(2)}, u32[]{:S(2)}) collective-permute-start(bf16[128,128]{0,1:T(8,128)(2,1)S(1)} %get-tuple-element.591), channel_id=1, source_target_pairs={{0,254},{2,0},{4,2},{6,4},{8,6},{10,8},{12,10},{14,12},{16,14},{18... | collective-permute-start | bytes 98312 | tf_op jit(solution)/shard_map/ppermute | solution.py:15
  127.8 8.5 %collective-permute-start.10 = (bf16[128,128]{0,1:T(8,128)(2,1)S(1)}, bf16[128,128]{0,1:T(8,128)(2,1)S(1)}, u32[]{:S(2)}, u32[]{:S(2)}) collective-permute-start(bf16[128,128]{0,1:T(8,128)(2,1)S(1)} %get-tuple-element.590), channel_id=1, source_target_pairs={{0,4},{2,6},{4,8},{6,10},{8,12},{10,14},{12,16},{14,18},{16,20},{1... | collective-permute-start | bytes 98312 | tf_op jit(solution)/shard_map/ppermute | solution.py:15
  127.8 8.5 %collective-permute-start.11 = (bf16[128,128]{0,1:T(8,128)(2,1)S(1)}, bf16[128,128]{0,1:T(8,128)(2,1)S(1)}, u32[]{:S(2)}, u32[]{:S(2)}) collective-permute-start(bf16[128,128]{0,1:T(8,128)(2,1)S(1)} %get-tuple-element.589), channel_id=1, source_target_pairs={{0,252},{2,254},{4,0},{6,2},{8,4},{10,6},{12,8},{14,10},{16,12},{1... | collective-permute-start | bytes 98312 | tf_op jit(solution)/shard_map/ppermute | solution.py:15
  200.2 15.4 %copy-start.12 = (bf16[1,128,2,64]{1,3,2,0:T(8,128)(2,1)S(1)}, bf16[1,128,2,64]{1,3,2,0:T(8,128)(2,1)}, u32[]{:S(2)}) copy-start(bf16[1,128,2,64]{1,3,2,0:T(8,128)(2,1)} %get-tuple-element.582) | copy-start | bytes 98308
  200.2 23.9 %copy-start.3 = (f32[1536,128]{1,0:T(8,128)S(1)}, f32[1536,128]{1,0:T(8,128)}, u32[]{:S(2)}) copy-start(f32[1536,128]{1,0:T(8,128)} %get-tuple-element.187) | copy-start | bytes 2359300
  201.4 14.4 %collective-permute-start.12 = (bf16[128,128]{1,0:T(8,128)(2,1)S(1)}, bf16[128,128]{1,0:T(8,128)(2,1)S(1)}, u32[]{:S(2)}, u32[]{:S(2)}) collective-permute-start(bf16[128,128]{1,0:T(8,128)(2,1)S(1)} %get-tuple-element.568), channel_id=1, source_target_pairs={{0,254},{2,0},{4,2},{6,4},{8,6},{10,8},{12,10},{14,12},{16,14},{18... | collective-permute-start | bytes 98312 | tf_op jit(solution)/shard_map/ppermute | solution.py:15
  202.3 13.5 %collective-permute-start.13 = (bf16[128,128]{1,0:T(8,128)(2,1)S(1)}, bf16[128,128]{1,0:T(8,128)(2,1)S(1)}, u32[]{:S(2)}, u32[]{:S(2)}) collective-permute-start(bf16[128,128]{1,0:T(8,128)(2,1)S(1)} %get-tuple-element.571), channel_id=1, source_target_pairs={{0,2},{2,4},{4,6},{6,8},{8,10},{10,12},{12,14},{14,16},{16,18},{18... | collective-permute-start | bytes 98312 | tf_op jit(solution)/shard_map/ppermute | solution.py:15
  203.0 13.6 %collective-permute-start.14 = (bf16[128,128]{1,0:T(8,128)(2,1)S(1)}, bf16[128,128]{1,0:T(8,128)(2,1)S(1)}, u32[]{:S(2)}, u32[]{:S(2)}) collective-permute-start(bf16[128,128]{1,0:T(8,128)(2,1)S(1)} %get-tuple-element.570), channel_id=1, source_target_pairs={{0,252},{2,254},{4,0},{6,2},{8,4},{10,6},{12,8},{14,10},{16,12},{1... | collective-permute-start | bytes 98312 | tf_op jit(solution)/shard_map/ppermute | solution.py:15
  215.6 8.5 %collective-permute-start.15 = (bf16[128,128]{1,0:T(8,128)(2,1)S(1)}, bf16[128,128]{1,0:T(8,128)(2,1)S(1)}, u32[]{:S(2)}, u32[]{:S(2)}) collective-permute-start(bf16[128,128]{1,0:T(8,128)(2,1)S(1)} %get-tuple-element.569), channel_id=1, source_target_pairs={{0,4},{2,6},{4,8},{6,10},{8,12},{10,14},{12,16},{14,18},{16,20},{1... | collective-permute-start | bytes 98312 | tf_op jit(solution)/shard_map/ppermute | solution.py:15
  215.8 17.2 %copy-start.8 = (bf16[1,128,2,64]{1,3,2,0:T(8,128)(2,1)S(1)}, bf16[1,128,2,64]{1,3,2,0:T(8,128)(2,1)}, u32[]{:S(2)}) copy-start(bf16[1,128,2,64]{1,3,2,0:T(8,128)(2,1)} %get-tuple-element.581) | copy-start | bytes 98308
  215.8 17.2 %copy-start.10 = (bf16[1,2,64,128]{3,2,0,1:T(8,128)(2,1)S(1)}, bf16[1,2,64,128]{3,2,0,1:T(8,128)(2,1)}, u32[]{:S(2)}) copy-start(bf16[1,2,64,128]{3,2,0,1:T(8,128)(2,1)} %get-tuple-element.602) | copy-start | bytes 98308
  236.2 8.8 %collective-permute-start.16 = (bf16[128,128]{0,1:T(8,128)(2,1)S(1)}, bf16[128,128]{0,1:T(8,128)(2,1)S(1)}, u32[]{:S(2)}, u32[]{:S(2)}) collective-permute-start(bf16[128,128]{0,1:T(8,128)(2,1)S(1)} %get-tuple-element.588), channel_id=1, source_target_pairs={{0,2},{2,4},{4,6},{6,8},{8,10},{10,12},{12,14},{14,16},{16,18},{18... | collective-permute-start | bytes 98312 | tf_op jit(solution)/shard_map/ppermute | solution.py:15
  236.3 8.7 %collective-permute-start.17 = (bf16[128,128]{0,1:T(8,128)(2,1)S(1)}, bf16[128,128]{0,1:T(8,128)(2,1)S(1)}, u32[]{:S(2)}, u32[]{:S(2)}) collective-permute-start(bf16[128,128]{0,1:T(8,128)(2,1)S(1)} %get-tuple-element.587), channel_id=1, source_target_pairs={{0,254},{2,0},{4,2},{6,4},{8,6},{10,8},{12,10},{14,12},{16,14},{18... | collective-permute-start | bytes 98312 | tf_op jit(solution)/shard_map/ppermute | solution.py:15
  237.8 8.5 %collective-permute-start.18 = (bf16[128,128]{0,1:T(8,128)(2,1)S(1)}, bf16[128,128]{0,1:T(8,128)(2,1)S(1)}, u32[]{:S(2)}, u32[]{:S(2)}) collective-permute-start(bf16[128,128]{0,1:T(8,128)(2,1)S(1)} %get-tuple-element.586), channel_id=1, source_target_pairs={{0,4},{2,6},{4,8},{6,10},{8,12},{10,14},{12,16},{14,18},{16,20},{1... | collective-permute-start | bytes 98312 | tf_op jit(solution)/shard_map/ppermute | solution.py:15
  237.8 8.5 %collective-permute-start.19 = (bf16[128,128]{0,1:T(8,128)(2,1)S(1)}, bf16[128,128]{0,1:T(8,128)(2,1)S(1)}, u32[]{:S(2)}, u32[]{:S(2)}) collective-permute-start(bf16[128,128]{0,1:T(8,128)(2,1)S(1)} %get-tuple-element.585), channel_id=1, source_target_pairs={{0,252},{2,254},{4,0},{6,2},{8,4},{10,6},{12,8},{14,10},{16,12},{1... | collective-permute-start | bytes 98312 | tf_op jit(solution)/shard_map/ppermute | solution.py:15
  257.8 3.2 copy-start.6
  265.6 3.2 copy-start.6
  273.3 3.2 copy-start.6
  281.0 3.2 copy-start.6
  288.8 3.2 copy-start.6
  296.5 3.2 copy-start.6
  304.3 3.2 copy-start.6
  307.5 25.1 %copy-start.1 = (bf16[8,512,128]{2,1,0:T(8,128)(2,1)}, bf16[8,512,128]{2,1,0:T(8,128)(2,1)S(1)}, u32[]{:S(2)}) copy-start(bf16[8,512,128]{2,1,0:T(8,128)(2,1)S(1)} %get-tuple-element.190) | copy-start | bytes 3145732
  307.5 15.7 %copy-start.11 = (bf16[1,128,2,64]{1,3,2,0:T(8,128)(2,1)S(1)}, bf16[1,128,2,64]{1,3,2,0:T(8,128)(2,1)}, u32[]{:S(2)}) copy-start(bf16[1,128,2,64]{1,3,2,0:T(8,128)(2,1)} %get-tuple-element.580) | copy-start | bytes 98308
  307.5 24.2 %copy-start.2 = (f32[1536,128]{1,0:T(8,128)S(1)}, f32[1536,128]{1,0:T(8,128)}, u32[]{:S(2)}) copy-start(f32[1536,128]{1,0:T(8,128)} %get-tuple-element.189) | copy-start | bytes 2359300
  309.1 14.4 %collective-permute-start.20 = (bf16[128,128]{1,0:T(8,128)(2,1)S(1)}, bf16[128,128]{1,0:T(8,128)(2,1)S(1)}, u32[]{:S(2)}, u32[]{:S(2)}) collective-permute-start(bf16[128,128]{1,0:T(8,128)(2,1)S(1)} %get-tuple-element.564), channel_id=1, source_target_pairs={{0,254},{2,0},{4,2},{6,4},{8,6},{10,8},{12,10},{14,12},{16,14},{18... | collective-permute-start | bytes 98312 | tf_op jit(solution)/shard_map/ppermute | solution.py:15
  309.9 13.6 %collective-permute-start.21 = (bf16[128,128]{1,0:T(8,128)(2,1)S(1)}, bf16[128,128]{1,0:T(8,128)(2,1)S(1)}, u32[]{:S(2)}, u32[]{:S(2)}) collective-permute-start(bf16[128,128]{1,0:T(8,128)(2,1)S(1)} %get-tuple-element.567), channel_id=1, source_target_pairs={{0,2},{2,4},{4,6},{6,8},{8,10},{10,12},{12,14},{14,16},{16,18},{18... | collective-permute-start | bytes 98312 | tf_op jit(solution)/shard_map/ppermute | solution.py:15
  310.6 13.6 %collective-permute-start.22 = (bf16[128,128]{1,0:T(8,128)(2,1)S(1)}, bf16[128,128]{1,0:T(8,128)(2,1)S(1)}, u32[]{:S(2)}, u32[]{:S(2)}) collective-permute-start(bf16[128,128]{1,0:T(8,128)(2,1)S(1)} %get-tuple-element.566), channel_id=1, source_target_pairs={{0,252},{2,254},{4,0},{6,2},{8,4},{10,6},{12,8},{14,10},{16,12},{1... | collective-permute-start | bytes 98312 | tf_op jit(solution)/shard_map/ppermute | solution.py:15
  323.2 8.5 %collective-permute-start.23 = (bf16[128,128]{1,0:T(8,128)(2,1)S(1)}, bf16[128,128]{1,0:T(8,128)(2,1)S(1)}, u32[]{:S(2)}, u32[]{:S(2)}) collective-permute-start(bf16[128,128]{1,0:T(8,128)(2,1)S(1)} %get-tuple-element.565), channel_id=1, source_target_pairs={{0,4},{2,6},{4,8},{6,10},{8,12},{10,14},{12,16},{14,18},{16,20},{1... | collective-permute-start | bytes 98312 | tf_op jit(solution)/shard_map/ppermute | solution.py:15
  323.4 17.1 %copy-start.9 = (bf16[1,2,64,128]{3,2,0,1:T(8,128)(2,1)S(1)}, bf16[1,2,64,128]{3,2,0,1:T(8,128)(2,1)}, u32[]{:S(2)}) copy-start(bf16[1,2,64,128]{3,2,0,1:T(8,128)(2,1)} %get-tuple-element.601) | copy-start | bytes 98308
  (10 other events, 17.1 us)
where the time goes:
time: 347 us; the launch traced here: 344 us
  matrix products  168 us (48%)
  starting transfers between devices  78.3 us (23%)
  blocking collectives  29.3 us (8%)
  waiting for transfers between devices  26.4 us (8%)
  other arithmetic  24.6 us (7%)
  local copies, waits for them, and re-layouts  13.4 us (4%)
    dot_general x105, matrix products, product(): jnp.dot(first_operand, second_operand, preferred_element_type=jnp.float32)  107 us
    ppermute x24, starting transfers between devices, from_behind(): lax.ppermute(array, axis, [(i, (i + by) % length) for i in range(length)])  69.9 us
    dot_general x24, matrix products, column_sum(): lax.dot_general(table, values, (((0,), (0,)), ((), ())), preferred_elemen...  58.9 us
    ppermute x24, waiting for transfers between devices, from_behind(): lax.ppermute(array, axis, [(i, (i + by) % length) for i in range(length)])  26.4 us
    all_to_all x3, blocking collectives, sum_at_owner(): lax.all_to_all(in_blocks(array, dim, length), axis, 0, 0, tiled=True)  21.3 us
    dynamic_update_slice x24, other arithmetic, local(): summed, renewed_blocks = lax.scan(edge_block, start_sums, edge_pieces)  8.73 us
    all_to_all x2, starting transfers between devices, copy_for_each(): return lax.all_to_all(copies, axis, split_axis=0, concat_axis=0, tiled=True)  8.4 us
  transfers between devices with their start and end apart: 26, of which 7 were waited for; matrix products, arithmetic and copies ran while one was open for 21% of the time, Pallas kernels for 0%

commit v1 on v0

v1 whole, which is shorter than its diff:
```python
import functools

import jax
import jax.numpy as jnp
from jax import lax
from jax.experimental import pallas as pl
from jax.experimental.pallas import tpu as pltpu
from jax.sharding import PartitionSpec as P

LAYERS = 3
OFFSETS = (1, -1, 2, -2)
NORM_FLOOR = 0.25
MESH = pl.DeviceIdType.MESH
F32 = jnp.float32
BF16 = jnp.bfloat16


def mm(a, b):
    return jnp.dot(a, b, preferred_element_type=F32)


def layer_norm(values):
    centre = jnp.mean(values, axis=-1, keepdims=True)
    centred = values - centre
    spread = jnp.mean(centred * centred, axis=-1, keepdims=True)
    return centred * lax.rsqrt(spread + NORM_FLOOR)


def hot(match):
    return jnp.where(match, 1.0, 0.0).astype(BF16)


def column(row, width):
    return jnp.transpose(jnp.broadcast_to(row, (width, width)))


def pick_half(both, high):
    return jnp.where(high, both[:, 128:], both[:, :128])


def kernel(
    doms, tile,
    x_in, e_hbm, snd, rcv, cnt, sidx, w_in, w_out, n_in, n_out,
    x_out, e_out,
    x, e, hot_s, hot_r, hot_t, code_s, code_r, acc, msg2,
    pick, pick_t, pick_hi, tab_s, tab_r, halo_sum,
    w_in_peer, n_in_peer, w_out_full, n_out_full, w_sr, w_e2, w_o2, n_in_full,
    fwd_buf, halo, ret_buf, ret, own_buf, own_peer,
    e_sem, eo_sem, w_send, w_recv, fwd_send, fwd_recv, ret_send, ret_recv,
    rel_send, rel_recv, own_send, own_recv,
):
    p = lax.axis_index("dom")
    t = lax.axis_index("tp")
    peer = (p, 1 - t)
    to = [(lax.rem(p + o + doms, doms), t) for o in OFFSETS]
    back = [(lax.rem(p - o + doms, doms), t) for o in OFFSETS]
    edges = e.shape[0]
    tiles = edges // tile
    half = tile // 2

    barrier = pltpu.get_barrier_semaphore()
    for other in to + [peer]:
        pl.semaphore_signal(barrier, inc=1, device_id=other, device_id_type=MESH)

    load_e = pltpu.make_async_copy(e_hbm, e, e_sem)
    load_e.start()

    def remote(src, dst, send, recv, device):
        return pltpu.make_async_remote_copy(
            src_ref=src, dst_ref=dst, send_sem=send, recv_sem=recv,
            device_id=device, device_id_type=MESH,
        )

    def fwd_copy(layer, k):
        return remote(fwd_buf.at[layer, k], halo.at[layer, k],
                      fwd_send.at[layer, k], fwd_recv.at[layer, k], to[k])

    def ret_copy(layer, k):
        return remote(ret_buf.at[layer, k], ret.at[layer, t, k],
                      ret_send.at[layer, k], ret_recv.at[layer, k], back[k])

    def relay_copy(layer, k):
        return remote(ret.at[layer, t, k], ret.at[layer, t, k],
                      rel_send.at[layer, k], rel_recv.at[layer, k], peer)

    def own_copy(layer):
        return remote(own_buf.at[layer], own_peer.at[layer],
                      own_send.at[layer], own_recv.at[layer], peer)

    rows64 = pl.ds(pl.multiple_of(t * 64, 64), 64)
    weight_copies = [
        remote(w_in, w_in_peer, w_send.at[0], w_recv.at[0], peer),
        remote(n_in, n_in_peer, w_send.at[1], w_recv.at[1], peer),
        remote(w_out, w_out_full.at[:, rows64, :], w_send.at[2], w_recv.at[2], peer),
        remote(n_out, n_out_full.at[:, rows64, :], w_send.at[3], w_recv.at[3], peer),
    ]

    lane = lax.broadcasted_iota(jnp.int32, (128, 128), 1)
    sub = lax.broadcasted_iota(jnp.int32, (128, 128), 0)

    for k in range(4):
        row = sidx[pl.ds(k, 1), :]
        wide = column(row, 128)
        rows = pl.ds(k * 128, 128)
        low = jnp.where(wide < 0, -1, wide & 511)
        low_row = jnp.broadcast_to(jnp.where(row < 0, -1, row & 511), (128, 128))
        pick_hi[rows, :] = jnp.where(wide >= 512, 1, 0)
        for g in range(4):
            pick[rows, g * 128 : (g + 1) * 128] = hot(low == lane + g * 128)
            pick_t[g * 128 : (g + 1) * 128, rows] = hot(low_row == sub + g * 128)

    def fill_fwd(layer):
        for k in range(4):
            rows = pl.ds(k * 128, 128)
            table = jnp.concatenate([x[0:512, :], x[512:1024, :]], axis=1)
            both = mm(pick[rows, :], table)
            fwd_buf[layer, k, :, :] = pick_half(both, pick_hi[rows, :] > 0).astype(BF16)

    x[...] = x_in[...]
    fill_fwd(0)
    pl.semaphore_wait(barrier, 5)
    for k in range(4):
        fwd_copy(0, k).start()
    for copy in weight_copies:
        copy.start()

    live = cnt[0]

    def split(row):
        own = row < 1024
        low = jnp.where(own, row & 511, 512 + (row & 255))
        high = jnp.where(own, row >> 9, (row >> 8) & 1)
        return low, high

    def build(c, carry):
        rows = pl.ds(pl.multiple_of(c * 128, 128), 128)
        low, high = split(snd[pl.ds(c, 1), :])
        both = column(low + high * 1024, 128)
        low_c = both & 1023
        code_s[rows, :] = both >> 10
        for g in range(6):
            hot_s[rows, g * 128 : (g + 1) * 128] = hot(low_c == lane + g * 128)
        low, high = split(rcv[pl.ds(c, 1), :])
        both = column(low + high * 1024, 128)
        low_c = both & 1023
        code_r[rows, :] = jnp.where(sub + c * 128 < live, both >> 10, 2)
        low_b = jnp.broadcast_to(low, (128, 128))
        for g in range(6):
            hot_r[rows, g * 128 : (g + 1) * 128] = hot(low_c == lane + g * 128)
            hot_t[g * 128 : (g + 1) * 128, rows] = hot(low_b == sub + g * 128)
        return carry

    lax.fori_loop(0, edges // 128, build, 0)

    w_out_full[:, rows64, :] = w_out[...]
    n_out_full[:, rows64, :] = n_out[...]
    for copy in weight_copies:
        copy.wait()
    first = t == 0

    def joined(mine, theirs):
        left = jnp.where(first, mine.astype(F32), theirs.astype(F32))
        right = jnp.where(first, theirs.astype(F32), mine.astype(F32))
        return jnp.concatenate([left, right], axis=-1).astype(BF16)

    w_e2[...] = jnp.zeros_like(w_e2)
    w_o2[...] = jnp.zeros_like(w_o2)
    for s in range(LAYERS):
        for part in range(3):
            rows = pl.ds(part * 128, 128)
            full = joined(w_in[s, rows, :], w_in_peer[s, rows, :])
            if part == 0:
                w_e2[s, 0:128, 0:128] = full
                w_e2[s, 128:256, 128:256] = full
            else:
                w_sr[s, :, (part - 1) * 128 : part * 128] = full
        n_in_full[s, :, :] = joined(n_in[s, :, :], n_in_peer[s, :, :])
        full = w_out_full[s, :, :]
        w_o2[s, 0:128, 0:128] = full
        w_o2[s, 128:256, 128:256] = full
    load_e.wait()

    def layer_step(s, carry):
        for h in range(2):
            proj = mm(x[h * 512 : (h + 1) * 512, :], w_sr[s, :, :]).astype(BF16)
            tab_s[0:512, h * 128 : (h + 1) * 128] = proj[:, 0:128]
            tab_r[0:512, h * 128 : (h + 1) * 128] = proj[:, 128:256]

        def owned_pass(j, c):
            start = pl.multiple_of(j * tile, tile)
            rows = pl.ds(start, tile)
            pair = jnp.concatenate(
                [e[pl.ds(start, half), :],
                 e[pl.ds(pl.multiple_of(start + half, half), half), :]], axis=1)
            lin = mm(pair, w_e2[s, :, :])
            lin = jnp.concatenate([lin[:, 0:128], lin[:, 128:256]], axis=0)
            from_s = mm(hot_s[rows, 0:512], tab_s[0:512, :])
            lin = lin + pick_half(from_s, code_s[rows, :] > 0)
            from_r = mm(hot_r[rows, 0:512], tab_r[0:512, :])
            acc[rows, :] = lin + pick_half(from_r, code_r[rows, :] == 1)
            return c

        lax.fori_loop(0, tiles, owned_pass, 0)

        for k in range(4):
            fwd_copy(s, k).wait_recv()
        for h in range(2):
            held = jnp.concatenate([halo[s, 2 * h, :, :], halo[s, 2 * h + 1, :, :]], axis=0)
            proj = mm(held, w_sr[s, :, :]).astype(BF16)
            tab_s[512:768, h * 128 : (h + 1) * 128] = proj[:, 0:128]
            tab_r[512:768, h * 128 : (h + 1) * 128] = proj[:, 128:256]
        halo_sum[...] = jnp.zeros_like(halo_sum)

        def halo_pass(j, c):
            start = pl.multiple_of(j * tile, tile)
            rows = pl.ds(start, tile)
            from_s = mm(hot_s[rows, 512:768], tab_s[512:768, :])
            from_r = mm(hot_r[rows, 512:768], tab_r[512:768, :])
            code = code_r[rows, :]
            lin = acc[rows, :] + pick_half(from_s, code_s[rows, :] > 0)
            lin = lin + pick_half(from_r, code == 1)
            hidden = jnp.maximum(lin, 0.0).astype(BF16)
            pair = jnp.concatenate([hidden[0:half, :], hidden[half:tile, :]], axis=1)
            out = mm(pair, w_o2[s, :, :])
            out = layer_norm(jnp.concatenate([out[:, 0:128], out[:, 128:256]], axis=0))
            low = jnp.where(code == 0, out, 0.0).astype(BF16)
            high = jnp.where(code == 1, out, 0.0).astype(BF16)
            both = jnp.concatenate([low, high], axis=1)
            msg2[rows, :] = both
            message = low.astype(F32) + high.astype(F32)
            e[rows, :] = (e[rows, :].astype(F32) + message).astype(BF16)
            halo_sum[...] += mm(hot_t[512:768, rows], both)

            @pl.when(s == LAYERS - 1)
            def _():
                pltpu.make_async_copy(e.at[rows, :], e_out.at[rows, :], eo_sem.at[j]).start()

            return c

        lax.fori_loop(0, tiles, halo_pass, 0)

        for k in range(4):
            rows = pl.ds((k % 2) * 128, 128)
            lanes = pl.ds((k // 2) * 128, 128)
            ret_buf[s, k, :, :] = halo_sum[rows, lanes].astype(BF16)
            ret_copy(s, k).start()

        owned = mm(hot_t[0:512, :], msg2[...]).astype(BF16)
        own_buf[s, 0:512, :] = owned[:, 0:128]
        own_buf[s, 512:1024, :] = owned[:, 128:256]
        own_copy(s).start()

        for k in range(4):
            ret_copy(s, k).wait_recv()
            relay_copy(s, k).start()
        own_copy(s).wait_recv()
        for k in range(4):
            relay_copy(s, k).wait_recv()

        back_sum = jnp.zeros((512, 256), F32)
        for source in range(2):
            for k in range(4):
                rows = pl.ds(k * 128, 128)
                high = pick_hi[rows, :] > 0
                block = ret[s, source, k, :, :].astype(F32)
                low_part = jnp.where(high, 0.0, block).astype(BF16)
                high_part = jnp.where(high, block, 0.0).astype(BF16)
                msg2[pl.ds(source * 512 + k * 128, 128), :] = jnp.concatenate(
                    [low_part, high_part], axis=1)
        back_sum = mm(pick_t[...], msg2[0:512, :]) + mm(pick_t[...], msg2[512:1024, :])
        for h in range(2):
            rows = pl.ds(h * 512, 512)
            now = x[rows, :]
            both = own_buf[s, rows, :].astype(F32) + own_peer[s, rows, :].astype(F32)
            total = (both + back_sum[:, h * 128 : (h + 1) * 128]).astype(BF16)
            lin = mm(jnp.concatenate([now, total], axis=1), n_in_full[s, :, :])
            hidden = jnp.maximum(lin, 0.0).astype(BF16)
            update = layer_norm(mm(hidden, n_out_full[s, :, :]))
            x[rows, :] = (now.astype(F32) + update).astype(BF16)

        @pl.when(s < LAYERS - 1)
        def _():
            fill_fwd(s + 1)
            for k in range(4):
                fwd_copy(s + 1, k).start()

        return carry

    lax.fori_loop(0, LAYERS, layer_step, 0)
    x_out[...] = x[...]

    for s in range(LAYERS):
        for k in range(4):
            fwd_copy(s, k).wait_send()
            ret_copy(s, k).wait_send()
            relay_copy(s, k).wait_send()
        own_copy(s).wait_send()
    for j in range(tiles):
        rows = pl.ds(j * tile, tile)
        pltpu.make_async_copy(e.at[rows, :], e_out.at[rows, :], eo_sem.at[j]).wait()


def local(
    doms,
    node_latent, edge_latent, edge_sender, edge_receiver, edge_count, send_index,
    edge_in, edge_out, node_in, node_out,
):
    edges = edge_latent.shape[0]
    tile = min(512, edges)
    tiles = edges // tile
    vmem = pl.BlockSpec(memory_space=pltpu.VMEM)
    anywhere = pl.BlockSpec(memory_space=pl.ANY)
    dma = pltpu.SemaphoreType.DMA
    scratch = [
        pltpu.VMEM((1024, 128), BF16),
        pltpu.VMEM((edges, 128), BF16),
        pltpu.VMEM((edges, 768), BF16),
        pltpu.VMEM((edges, 768), BF16),
        pltpu.VMEM((768, edges), BF16),
        pltpu.VMEM((edges, 128), jnp.int32),
        pltpu.VMEM((edges, 128), jnp.int32),
        pltpu.VMEM((edges, 128), F32),
        pltpu.VMEM((max(edges, 1024), 256), BF16),
        pltpu.VMEM((512, 512), BF16),
        pltpu.VMEM((512, 512), BF16),
        pltpu.VMEM((512, 128), jnp.int32),
        pltpu.VMEM((768, 256), BF16),
        pltpu.VMEM((768, 256), BF16),
        pltpu.VMEM((256, 256), F32),
        pltpu.VMEM(edge_in.shape, BF16),
        pltpu.VMEM(node_in.shape, BF16),
        pltpu.VMEM((LAYERS, 128, 128), BF16),
        pltpu.VMEM((LAYERS, 128, 128), BF16),
        pltpu.VMEM((LAYERS, 128, 256), BF16),
        pltpu.VMEM((LAYERS, 256, 256), BF16),
        pltpu.VMEM((LAYERS, 256, 256), BF16),
        pltpu.VMEM((LAYERS, 256, 128), BF16),
        pltpu.VMEM((LAYERS, 4, 128, 128), BF16),
        pltpu.VMEM((LAYERS, 4, 128, 128), BF16),
        pltpu.VMEM((LAYERS, 4, 128, 128), BF16),
        pltpu.VMEM((LAYERS, 2, 4, 128, 128), BF16),
        pltpu.VMEM((LAYERS, 1024, 128), BF16),
        pltpu.VMEM((LAYERS, 1024, 128), BF16),
        dma, dma((tiles,)), dma((4,)), dma((4,)),
        dma((LAYERS, 4)), dma((LAYERS, 4)), dma((LAYERS, 4)), dma((LAYERS, 4)),
        dma((LAYERS, 4)), dma((LAYERS, 4)), dma((LAYERS,)), dma((LAYERS,)),
    ]
    return pl.pallas_call(
        functools.partial(kernel, doms, tile),
        out_shape=(
            jax.ShapeDtypeStruct(node_latent.shape, BF16),
            jax.ShapeDtypeStruct(edge_latent.shape, BF16),
        ),
        in_specs=[vmem, anywhere, vmem, vmem, pl.BlockSpec(memory_space=pltpu.SMEM)]
        + [vmem] * 5,
        out_specs=(vmem, anywhere),
        scratch_shapes=scratch,
        compiler_params=pltpu.CompilerParams(
            collective_id=0, has_side_effects=True, vmem_limit_bytes=60 << 20,
        ),
    )(
        node_latent, edge_latent,
        edge_sender.reshape(-1, 128), edge_receiver.reshape(-1, 128), edge_count,
        send_index.reshape(4, 128), edge_in, edge_out, node_in, node_out,
    )


def solution(mesh):
    return jax.shard_map(
        functools.partial(local, mesh.shape["dom"]),
        mesh=mesh,
        in_specs=(
            P("dom", None),
            P(("dom", "tp"), None),
            P(("dom", "tp")),
            P(("dom", "tp")),
            P(("dom", "tp")),
            P("dom", None, None),
            P(None, None, "tp"),
            P(None, "tp", None),
            P(None, None, "tp"),
            P(None, "tp", None),
        ),
        out_specs=(P("dom", None), P(("dom", "tp"), None)),
        check_vma=False,
    )
```

time: 347 us -> 93.4 us (0.27)
  the two profiles are of different devices: /device:TPU:3 before, /device:TPU:1 now
where the time goes in v1:
time: 93.4 us; the launch traced here: 93.2 us
  Pallas kernels  85.3 us (91%)
  local copies, waits for them, and re-layouts  6.57 us (7%)
  between operations  1.29 us (1%)
    pallas_call x1, Pallas kernels, local(): pl.pallas_call(functools.partial(kernel, doms, tile), out_shape=(jax.Shap...  85.3 us
    unnamed x6, local copies, waits for them, and re-layouts  6.57 us

profile of v1, /device:TPU:1, one launch (start us, length us, event | category | flops | bytes accessed | tf_op | source)
XLA Modules:
  0.0 93.2 jit_solution(1480518629675191259)
XLA Ops:
  1.3 0.0 copy-start
  1.3 1.7 %copy.13.n_in = bf16[3,256,64]{2,1,0:T(8,128)(2,1)} copy(bf16[3,256,64]{1,2,0:T(8,128)(2,1)} %param.18) | data formatting | bytes 196608 | tf_op args[8]
  3.0 0.0 copy-done
  3.0 0.9 copy.12.w_in
  3.9 85.3 %shard_map.113 = (bf16[1024,128]{1,0:T(8,128)(2,1)}, bf16[4096,128]{1,0:T(8,128)(2,1)}) custom-call(bf16[1024,128]{1,0:T(8,128)(2,1)} %x_in.1, bf16[4096,128]{1,0:T(8,128)(2,1)} %e_hbm.1, s32[32,128]{1,0:T(8,128)} %bitcast.3, s32[32,128]{1,0:T(8,128)} %bitcast.4, s32[1]{0:T(128)S(6)} %copy.16.cnt, s32[4,128]{1,0:T(4,128)} %bitcast.5, ...), custom_call_target="tpu_custom_call" | custom-call | tf_op jit(solution)/shard_map/pallas_call | solution.py:348
  89.3 1.7 %copy.17 = bf16[1024,128]{1,0:T(8,128)(2,1)} copy(bf16[1024,128]{1,0:T(8,128)(2,1)} %get-tuple-element.4) | data formatting | bytes 524288
  90.9 2.3 %copy.18 = bf16[4096,128]{1,0:T(8,128)(2,1)} copy(bf16[4096,128]{1,0:T(8,128)(2,1)} %get-tuple-element.5) | data formatting | bytes 2097152
Async XLA Ops:
  1.3 1.8 %copy-start = (bf16[3,384,64]{1,2,0:T(8,128)(2,1)S(1)}, bf16[3,384,64]{1,2,0:T(8,128)(2,1)}, u32[]{:S(2)}) copy-start(bf16[3,384,64]{1,2,0:T(8,128)(2,1)} %param.16) | copy-start | bytes 442372

commit v2 on v1

v2 whole, which is shorter than its diff:
```python
import functools

import jax
import jax.numpy as jnp
from jax import lax
from jax.experimental import pallas as pl
from jax.experimental.pallas import tpu as pltpu
from jax.sharding import PartitionSpec as P

LAYERS = 3
OFFSETS = (1, -1, 2, -2)
NORM_FLOOR = 0.25
MESH = pl.DeviceIdType.MESH
F32 = jnp.float32
BF16 = jnp.bfloat16
I16 = jnp.int16
I32 = jnp.int32


def mm(a, b):
    return jnp.dot(a, b, preferred_element_type=F32)


def mm_t(a, b):
    return lax.dot_general(a, b, (((1,), (1,)), ((), ())), preferred_element_type=F32)


def beside(*parts):
    return jnp.concatenate(parts, axis=1)


def below(*parts):
    return jnp.concatenate(parts, axis=0)


def layer_norm(values):
    centre = jnp.mean(values, axis=-1, keepdims=True)
    centred = values - centre
    spread = jnp.mean(centred * centred, axis=-1, keepdims=True)
    return centred * lax.rsqrt(spread + NORM_FLOOR)


def hot(match):
    return jnp.where(match, jnp.ones((), BF16), jnp.zeros((), BF16))


def column(row):
    return jnp.transpose(jnp.broadcast_to(row, (128, 128)))


def pick_half(both, high):
    return jnp.where(high, both[:, 128:], both[:, :128])


def kernel(
    doms, tile,
    x_in, e_hbm, snd, rcv, cnt, sidx, w_in, w_out, n_in, n_out,
    x_out, e_out,
    x, e, hot_s, hot_r, hot_t, code_s, code_r, acc, msg2,
    pick, pick_t, pick_hi, tab_s, tab_r,
    w_in_t, n_in_t, w_out_full, n_out_full, w_sr_t, w_e2, w_o2,
    fwd_buf, halo, ret_buf, ret, own_buf, own_peer,
    e_sem, eo_sem, w_send, w_recv, fwd_send, fwd_recv, ret_send, ret_recv,
    rel_send, rel_recv, own_send, own_recv,
):
    p = lax.axis_index("dom")
    t = lax.axis_index("tp")
    peer = (p, 1 - t)
    to = [(lax.rem(p + o + doms, doms), t) for o in OFFSETS]
    back = [(lax.rem(p - o + doms, doms), t) for o in OFFSETS]
    edges = e.shape[0]
    tiles = edges // tile
    half = tile // 2
    chunks = tile // 128

    barrier = pltpu.get_barrier_semaphore()
    for other in to + [peer]:
        pl.semaphore_signal(barrier, inc=1, device_id=other, device_id_type=MESH)

    load_e = pltpu.make_async_copy(e_hbm, e, e_sem)
    load_e.start()

    def remote(src, dst, send, recv, device):
        return pltpu.make_async_remote_copy(
            src_ref=src, dst_ref=dst, send_sem=send, recv_sem=recv,
            device_id=device, device_id_type=MESH,
        )

    def fwd_copy(layer, k):
        return remote(fwd_buf.at[layer, k], halo.at[layer, k],
                      fwd_send.at[layer, k], fwd_recv.at[layer, k], to[k])

    def ret_copy(layer, k):
        return remote(ret_buf.at[layer, k], ret.at[layer, t, k],
                      ret_send.at[layer, k], ret_recv.at[layer, k], back[k])

    def relay_copy(layer, k):
        return remote(ret.at[layer, t, k], ret.at[layer, t, k],
                      rel_send.at[layer, k], rel_recv.at[layer, k], peer)

    def own_copy(layer):
        return remote(own_buf.at[layer], own_peer.at[layer],
                      own_send.at[layer], own_recv.at[layer], peer)

    rows64 = pl.ds(pl.multiple_of(t * 64, 64), 64)
    weight_copies = [
        remote(src, dst.at[:, rows64, :], w_send.at[i], w_recv.at[i], peer)
        for i, (src, dst) in enumerate(
            [(w_in, w_in_t), (w_out, w_out_full), (n_in, n_in_t), (n_out, n_out_full)])
    ]

    lane = lax.broadcasted_iota(I32, (128, 128), 1)
    sub = lax.broadcasted_iota(I32, (128, 128), 0)
    lane16 = lane.astype(I16)
    sub16 = sub.astype(I16)

    for k in range(4):
        row = sidx[pl.ds(k, 1), :]
        wide = column(row)
        rows = pl.ds(k * 128, 128)
        low = jnp.where(wide < 0, -1, wide & 511).astype(I16)
        low_row = jnp.broadcast_to(jnp.where(row < 0, -1, row & 511), (128, 128)).astype(I16)
        pick_hi[rows, :] = jnp.where(wide >= 512, 1, 0)
        for g in range(4):
            pick[g, rows, :] = hot(low == lane16 + I16(g * 128))
            pick_t[k, g * 128 : (g + 1) * 128, :] = hot(low_row == sub16 + I16(g * 128))

    def fill_fwd(layer):
        table = beside(x[0:512, :], x[512:1024, :])
        both = mm(beside(*[pick[g, :, :] for g in range(4)]), table)
        picked = pick_half(both, pick_hi[...] > 0).astype(BF16)
        for k in range(4):
            fwd_buf[layer, k, :, :] = picked[k * 128 : (k + 1) * 128, :]

    x[...] = x_in[...]
    fill_fwd(0)
    pl.semaphore_wait(barrier, 5)
    for k in (2, 3, 0, 1):
        fwd_copy(0, k).start()
    for copy in weight_copies:
        copy.start()
    for src, dst in [(w_in, w_in_t), (w_out, w_out_full), (n_in, n_in_t), (n_out, n_out_full)]:
        dst[:, rows64, :] = src[...]
    w_e2[...] = jnp.zeros_like(w_e2)
    w_o2[...] = jnp.zeros_like(w_o2)

    live = cnt[0, 0]

    def split(row):
        own = row < 1024
        low = jnp.where(own, row & 511, 512 + (row & 255))
        high = jnp.where(own, row >> 9, (row >> 8) & 1)
        return low, high

    def build(c, carry):
        rows = pl.ds(pl.multiple_of(c * 128, 128), 128)
        low, high = split(snd[pl.ds(c, 1), :])
        both = column(low + high * 1024)
        low_c = (both & 1023).astype(I16)
        code_s[rows, :] = both >> 10
        for g in range(6):
            hot_s[g, rows, :] = hot(low_c == lane16 + I16(g * 128))
        low, high = split(rcv[pl.ds(c, 1), :])
        both = column(low + high * 1024)
        low_c = (both & 1023).astype(I16)
        code_r[rows, :] = jnp.where(sub + c * 128 < live, both >> 10, 2)
        low_b = jnp.broadcast_to(low, (128, 128)).astype(I16)
        for g in range(6):
            hot_r[g, rows, :] = hot(low_c == lane16 + I16(g * 128))
            hot_t[c, g * 128 : (g + 1) * 128, :] = hot(low_b == sub16 + I16(g * 128))
        return carry

    lax.fori_loop(0, edges // 128, build, 0)

    for copy in weight_copies:
        copy.wait()
    for s in range(LAYERS):
        full = jnp.transpose(w_in_t[s, :, 0:128].astype(F32)).astype(BF16)
        w_e2[s, 0, 0:128, :] = full
        w_e2[s, 1, 128:256, :] = full
        w_sr_t[s, 0:128, :] = w_in_t[s, :, 128:256]
        w_sr_t[s, 128:256, :] = w_in_t[s, :, 256:384]
        full = w_out_full[s, :, :]
        w_o2[s, 0, 0:128, :] = full
        w_o2[s, 1, 128:256, :] = full
    load_e.wait()

    def layer_step(s, carry):
        for h in range(2):
            proj = mm_t(x[h * 512 : (h + 1) * 512, :], w_sr_t[s, :, :]).astype(BF16)
            tab_s[h, 0:512, :] = proj[:, 0:128]
            tab_r[h, 0:512, :] = proj[:, 128:256]

        def gather(hots, tab, rows, groups, table_rows):
            return mm(beside(*[hots[g, rows, :] for g in groups]),
                      beside(tab[0, table_rows, :], tab[1, table_rows, :]))

        def owned_pass(j, c):
            start = pl.multiple_of(j * tile, tile)
            rows = pl.ds(start, tile)
            pair = beside(e[pl.ds(start, half), :],
                          e[pl.ds(pl.multiple_of(start + half, half), half), :])
            lin = mm(pair, beside(w_e2[s, 0, :, :], w_e2[s, 1, :, :]))
            lin = below(lin[:, 0:128], lin[:, 128:256])
            owned_rows = pl.ds(0, 512)
            from_s = gather(hot_s, tab_s, rows, range(4), owned_rows)
            lin = lin + pick_half(from_s, code_s[rows, :] > 0)
            from_r = gather(hot_r, tab_r, rows, range(4), owned_rows)
            acc[rows, :] = lin + pick_half(from_r, code_r[rows, :] == 1)
            return c

        lax.fori_loop(0, tiles, owned_pass, 0)

        for k in range(4):
            fwd_copy(s, k).wait_recv()
        for h in range(2):
            held = below(halo[s, 2 * h, :, :], halo[s, 2 * h + 1, :, :])
            proj = mm_t(held, w_sr_t[s, :, :]).astype(BF16)
            tab_s[h, 512:768, :] = proj[:, 0:128]
            tab_r[h, 512:768, :] = proj[:, 128:256]

        halo_rows = pl.ds(512, 256)

        def hidden_of(j):
            rows = pl.ds(j * tile, tile)
            from_s = gather(hot_s, tab_s, rows, (4, 5), halo_rows)
            from_r = gather(hot_r, tab_r, rows, (4, 5), halo_rows)
            lin = acc[rows, :] + pick_half(from_s, code_s[rows, :] > 0)
            lin = lin + pick_half(from_r, code_r[rows, :] == 1)
            return jnp.maximum(lin, 0.0).astype(BF16)

        def message_of(j, hidden):
            rows = pl.ds(j * tile, tile)
            pair = beside(hidden[0:half, :], hidden[half:tile, :])
            out = mm(pair, beside(w_o2[s, 0, :, :], w_o2[s, 1, :, :]))
            out = layer_norm(below(out[:, 0:128], out[:, 128:256]))
            code = code_r[rows, :]
            low = jnp.where(code == 0, out, 0.0).astype(BF16)
            high = jnp.where(code == 1, out, 0.0).astype(BF16)
            msg2[0, rows, :] = low
            msg2[1, rows, :] = high
            message = low.astype(F32) + high.astype(F32)
            e[rows, :] = (e[rows, :].astype(F32) + message).astype(BF16)

            @pl.when(s == LAYERS - 1)
            def _():
                pltpu.make_async_copy(e.at[rows, :], e_out.at[rows, :], eo_sem.at[j]).start()

        hidden = hidden_of(0)
        for j in range(tiles):
            later = hidden_of(j + 1) if j + 1 < tiles else None
            message_of(j, hidden)
            hidden = later

        def scatter(row_from, row_to):
            return mm(beside(*[hot_t[c, row_from:row_to, :] for c in range(edges // 128)]),
                      beside(msg2[0, 0:edges, :], msg2[1, 0:edges, :]))

        sums = scatter(512, 768).astype(BF16)
        for k in range(4):
            ret_buf[s, k, :, :] = sums[(k % 2) * 128 : (k % 2 + 1) * 128,
                                       (k // 2) * 128 : (k // 2 + 1) * 128]
        for k in (2, 3, 0, 1):
            ret_copy(s, k).start()

        owned = scatter(0, 512).astype(BF16)
        own_buf[s, 0:512, :] = owned[:, 0:128]
        own_buf[s, 512:1024, :] = owned[:, 128:256]
        own_copy(s).start()

        for k in (0, 1, 2, 3):
            ret_copy(s, k).wait_recv()
            relay_copy(s, k).start()
        own_copy(s).wait_recv()
        for k in (0, 1, 2, 3):
            relay_copy(s, k).wait_recv()

        high = pick_hi[...] > 0
        places = beside(*[pick_t[k, :, :] for k in range(4)])
        back_sum = None
        for source in range(2):
            block = below(*[ret[s, source, k, :, :] for k in range(4)]).astype(F32)
            both = beside(jnp.where(high, 0.0, block), jnp.where(high, block, 0.0)).astype(BF16)
            part = mm(places, both)
            back_sum = part if back_sum is None else back_sum + part
        for h in range(2):
            rows = pl.ds(h * 512, 512)
            now = x[rows, :]
            both = own_buf[s, rows, :].astype(F32) + own_peer[s, rows, :].astype(F32)
            total = (both + back_sum[:, h * 128 : (h + 1) * 128]).astype(BF16)
            hidden = jnp.maximum(mm_t(beside(now, total), n_in_t[s, :, :]), 0.0).astype(BF16)
            update = layer_norm(mm(hidden, n_out_full[s, :, :]))
            x[rows, :] = (now.astype(F32) + update).astype(BF16)

        @pl.when(s < LAYERS - 1)
        def _():
            fill_fwd(s + 1)
            for k in (2, 3, 0, 1):
                fwd_copy(s + 1, k).start()

        return carry

    lax.fori_loop(0, LAYERS, layer_step, 0)
    x_out[...] = x[...]

    for s in range(LAYERS):
        for k in range(4):
            fwd_copy(s, k).wait_send()
            ret_copy(s, k).wait_send()
            relay_copy(s, k).wait_send()
        own_copy(s).wait_send()
    for j in range(tiles):
        rows = pl.ds(j * tile, tile)
        pltpu.make_async_copy(e.at[rows, :], e_out.at[rows, :], eo_sem.at[j]).wait()


def local(
    doms,
    node_latent, edge_latent, edge_sender, edge_receiver, edge_count, send_index,
    edge_in, edge_out, node_in, node_out,
):
    edges = edge_latent.shape[0]
    tile = min(512, edges)
    tiles = edges // tile
    vmem = pl.BlockSpec(memory_space=pltpu.VMEM)
    anywhere = pl.BlockSpec(memory_space=pl.ANY)
    dma = pltpu.SemaphoreType.DMA
    scratch = [
        pltpu.VMEM((1024, 128), BF16),
        pltpu.VMEM((edges, 128), BF16),
        pltpu.VMEM((6, edges, 128), BF16),
        pltpu.VMEM((6, edges, 128), BF16),
        pltpu.VMEM((edges // 128, 768, 128), BF16),
        pltpu.VMEM((edges, 128), I32),
        pltpu.VMEM((edges, 128), I32),
        pltpu.VMEM((edges, 128), F32),
        pltpu.VMEM((2, edges, 128), BF16),
        pltpu.VMEM((4, 512, 128), BF16),
        pltpu.VMEM((4, 512, 128), BF16),
        pltpu.VMEM((512, 128), I32),
        pltpu.VMEM((2, 768, 128), BF16),
        pltpu.VMEM((2, 768, 128), BF16),
        pltpu.VMEM((LAYERS, 128, 384), BF16),
        pltpu.VMEM((LAYERS, 128, 256), BF16),
        pltpu.VMEM((LAYERS, 128, 128), BF16),
        pltpu.VMEM((LAYERS, 128, 128), BF16),
        pltpu.VMEM((LAYERS, 256, 128), BF16),
        pltpu.VMEM((LAYERS, 2, 256, 128), BF16),
        pltpu.VMEM((LAYERS, 2, 256, 128), BF16),
        pltpu.VMEM((LAYERS, 4, 128, 128), BF16),
        pltpu.VMEM((LAYERS, 4, 128, 128), BF16),
        pltpu.VMEM((LAYERS, 4, 128, 128), BF16),
        pltpu.VMEM((LAYERS, 2, 4, 128, 128), BF16),
        pltpu.VMEM((LAYERS, 1024, 128), BF16),
        pltpu.VMEM((LAYERS, 1024, 128), BF16),
        dma, dma((tiles,)), dma((4,)), dma((4,)),
        dma((LAYERS, 4)), dma((LAYERS, 4)), dma((LAYERS, 4)), dma((LAYERS, 4)),
        dma((LAYERS, 4)), dma((LAYERS, 4)), dma((LAYERS,)), dma((LAYERS,)),
    ]
    return pl.pallas_call(
        functools.partial(kernel, doms, tile),
        out_shape=(
            jax.ShapeDtypeStruct(node_latent.shape, BF16),
            jax.ShapeDtypeStruct(edge_latent.shape, BF16),
        ),
        in_specs=[vmem, anywhere, vmem, vmem, pl.BlockSpec(memory_space=pltpu.SMEM)]
        + [vmem] * 5,
        out_specs=(vmem, anywhere),
        scratch_shapes=scratch,
        compiler_params=pltpu.CompilerParams(
            collective_id=0, has_side_effects=True, vmem_limit_bytes=60 << 20,
        ),
    )(
        node_latent, edge_latent,
        edge_sender.reshape(-1, 128), edge_receiver.reshape(-1, 128),
        edge_count.reshape(1, 1), send_index.reshape(4, 128),
        jnp.swapaxes(edge_in, 1, 2), edge_out, jnp.swapaxes(node_in, 1, 2), node_out,
    )


def solution(mesh):
    return jax.shard_map(
        functools.partial(local, mesh.shape["dom"]),
        mesh=mesh,
        in_specs=(
            P("dom", None),
            P(("dom", "tp"), None),
            P(("dom", "tp")),
            P(("dom", "tp")),
            P(("dom", "tp")),
            P("dom", None, None),
            P(None, None, "tp"),
            P(None, "tp", None),
            P(None, None, "tp"),
            P(None, "tp", None),
        ),
        out_specs=(P("dom", None), P(("dom", "tp"), None)),
        check_vma=False,
    )
```

time: 93.4 us -> 75.4 us (0.81)
  Pallas kernels: 85.3 us -> 70 us
  local copies, waits for them, and re-layouts: 6.57 us -> 3.93 us
    pallas_call x1, Pallas kernels: 85.3 us -> 70 us  [local(): pl.pallas_call(functools.partial(kernel, doms, tile), out_shape=(jax.Shap...]
    unnamed x6 -> x2, local copies, waits for them, and re-layouts: 6.57 us -> 3.93 us
where the time goes in v2:
time: 75.4 us; the launch traced here: 75.2 us
  Pallas kernels  70 us (93%)
  local copies, waits for them, and re-layouts  3.93 us (5%)
  between operations  1.29 us (2%)
    pallas_call x1, Pallas kernels, local(): pl.pallas_call(functools.partial(kernel, doms, tile), out_shape=(jax.Shap...  70 us
    unnamed x2, local copies, waits for them, and re-layouts  3.93 us

profile of v2, /device:TPU:1, one launch (start us, length us, event | category | flops | bytes accessed | tf_op | source)
XLA Modules:
  0.0 75.2 jit_solution(3234923586061842842)
XLA Ops:
  1.3 70.0 %shard_map.113 = (bf16[1024,128]{1,0:T(8,128)(2,1)}, bf16[4096,128]{1,0:T(8,128)(2,1)}) custom-call(bf16[1024,128]{1,0:T(8,128)(2,1)} %x_in.1, bf16[4096,128]{1,0:T(8,128)(2,1)} %e_hbm.1, s32[32,128]{1,0:T(8,128)} %bitcast.9, s32[32,128]{1,0:T(8,128)} %bitcast.10, s32[1,1]{1,0:T(1,128)} %bitcast.6.cnt, s32[4,128]{1,0:T(4,128)} %bitcast.11, ...), custom_call_target="tpu_custom_call" | custom-call | tf_op jit(solution)/shard_map/pallas_call | solution.py:360
  71.3 1.7 %copy.15 = bf16[1024,128]{1,0:T(8,128)(2,1)} copy(bf16[1024,128]{1,0:T(8,128)(2,1)} %get-tuple-element.4) | data formatting | bytes 524288
  73.0 2.3 %copy.16 = bf16[4096,128]{1,0:T(8,128)(2,1)} copy(bf16[4096,128]{1,0:T(8,128)(2,1)} %get-tuple-element.5) | data formatting | bytes 2097152

commit v3 on v2

--- a/solution.py
+++ b/solution.py
@@ -55,12 +55,12 @@
 def kernel(
     doms, tile,
     x_in, e_hbm, snd, rcv, cnt, sidx, w_in, w_out, n_in, n_out,
-    x_out, e_out,
-    x, e, hot_s, hot_r, hot_t, code_s, code_r, acc, msg2,
+    x, e,
+    hot_s, hot_r, hot_t, code, masks, acc, msg2,
     pick, pick_t, pick_hi, tab_s, tab_r,
     w_in_t, n_in_t, w_out_full, n_out_full, w_sr_t, w_e2, w_o2,
     fwd_buf, halo, ret_buf, ret, own_buf, own_peer,
-    e_sem, eo_sem, w_send, w_recv, fwd_send, fwd_recv, ret_send, ret_recv,
+    e_sem, w_send, w_recv, fwd_send, fwd_recv, ret_send, ret_recv,
     rel_send, rel_recv, own_send, own_recv,
 ):
     p = lax.axis_index("dom")
@@ -111,19 +111,29 @@
 
     lane = lax.broadcasted_iota(I32, (128, 128), 1)
     sub = lax.broadcasted_iota(I32, (128, 128), 0)
-    lane16 = lane.astype(I16)
-    sub16 = sub.astype(I16)
+    lane16 = lax.broadcasted_iota(I32, (16, 128), 1).astype(I16)
+    sub16 = lax.broadcasted_iota(I32, (16, 128), 0).astype(I16)
+    lane_of = [lane16 + I16(g * 128) for g in range(6)]
+
+    def hot_columns(ref, groups, start, low):
+        for i in range(8):
+            part = low[i * 16 : (i + 1) * 16, :]
+            for g in range(groups):
+                ref[g, pl.ds(start + i * 16, 16), :] = hot(part == lane_of[g])
+
+    def hot_rows(ref, c, count, low_row):
+        wide = jnp.broadcast_to(low_row, (16, 128)).astype(I16)
+        for i in range(count // 16):
+            ref[c, i * 16 : (i + 1) * 16, :] = hot(wide - I16(i * 16) == sub16)
 
     for k in range(4):
         row = sidx[pl.ds(k, 1), :]
         wide = column(row)
         rows = pl.ds(k * 128, 128)
         low = jnp.where(wide < 0, -1, wide & 511).astype(I16)
-        low_row = jnp.broadcast_to(jnp.where(row < 0, -1, row & 511), (128, 128)).astype(I16)
         pick_hi[rows, :] = jnp.where(wide >= 512, 1, 0)
-        for g in range(4):
-            pick[g, rows, :] = hot(low == lane16 + I16(g * 128))
-            pick_t[k, g * 128 : (g + 1) * 128, :] = hot(low_row == sub16 + I16(g * 128))
+        hot_columns(pick, 4, k * 128, low)
+        hot_rows(pick_t, k, 512, jnp.where(row < 0, -1, row & 511))
 
     def fill_fwd(layer):
         table = beside(x[0:512, :], x[512:1024, :])
@@ -153,21 +163,21 @@
         return low, high
 
     def build(c, carry):
-        rows = pl.ds(pl.multiple_of(c * 128, 128), 128)
+        start = pl.multiple_of(c * 128, 128)
+        rows = pl.ds(start, 128)
         low, high = split(snd[pl.ds(c, 1), :])
+        low_r, high_r = split(rcv[pl.ds(c, 1), :])
+        hot_rows(hot_t, c, 768, low_r)
         both = column(low + high * 1024)
-        low_c = (both & 1023).astype(I16)
-        code_s[rows, :] = both >> 10
-        for g in range(6):
-            hot_s[g, rows, :] = hot(low_c == lane16 + I16(g * 128))
-        low, high = split(rcv[pl.ds(c, 1), :])
-        both = column(low + high * 1024)
-        low_c = (both & 1023).astype(I16)
-        code_r[rows, :] = jnp.where(sub + c * 128 < live, both >> 10, 2)
-        low_b = jnp.broadcast_to(low, (128, 128)).astype(I16)
-        for g in range(6):
-            hot_r[g, rows, :] = hot(low_c == lane16 + I16(g * 128))
-            hot_t[c, g * 128 : (g + 1) * 128, :] = hot(low_b == sub16 + I16(g * 128))
+        both_r = column(low_r + high_r * 1024)
+        hot_columns(hot_s, 6, start, (both & 1023).astype(I16))
+        hot_columns(hot_r, 6, start, (both_r & 1023).astype(I16))
+        high = both >> 10
+        high_r = both_r >> 10
+        code[rows, :] = high + 2 * high_r
+        place = jnp.where(sub + start < live, high_r, 2)
+        masks[0, rows, :] = jnp.where(place == 0, 1.0, 0.0).astype(BF16)
+        masks[1, rows, :] = jnp.where(place == 1, 1.0, 0.0).astype(BF16)
         return carry
 
     lax.fori_loop(0, edges // 128, build, 0)
@@ -195,21 +205,20 @@
             return mm(beside(*[hots[g, rows, :] for g in groups]),
                       beside(tab[0, table_rows, :], tab[1, table_rows, :]))
 
-        def owned_pass(j, c):
-            start = pl.multiple_of(j * tile, tile)
-            rows = pl.ds(start, tile)
-            pair = beside(e[pl.ds(start, half), :],
-                          e[pl.ds(pl.multiple_of(start + half, half), half), :])
+        def with_picked(lin, from_s, from_r, rows):
+            held = code[rows, :]
+            lin = lin + pick_half(from_s, (held & 1) > 0)
+            return lin + pick_half(from_r, held > 1)
+
+        owned_rows = pl.ds(0, 512)
+        for j in range(tiles):
+            rows = pl.ds(j * tile, tile)
+            pair = beside(e[pl.ds(j * tile, half), :], e[pl.ds(j * tile + half, half), :])
             lin = mm(pair, beside(w_e2[s, 0, :, :], w_e2[s, 1, :, :]))
             lin = below(lin[:, 0:128], lin[:, 128:256])
-            owned_rows = pl.ds(0, 512)
             from_s = gather(hot_s, tab_s, rows, range(4), owned_rows)
-            lin = lin + pick_half(from_s, code_s[rows, :] > 0)
             from_r = gather(hot_r, tab_r, rows, range(4), owned_rows)
-            acc[rows, :] = lin + pick_half(from_r, code_r[rows, :] == 1)
-            return c
-
-        lax.fori_loop(0, tiles, owned_pass, 0)
+            acc[rows, :] = with_picked(lin, from_s, from_r, rows)
 
         for k in range(4):
             fwd_copy(s, k).wait_recv()
@@ -225,8 +234,7 @@
             rows = pl.ds(j * tile, tile)
             from_s = gather(hot_s, tab_s, rows, (4, 5), halo_rows)
             from_r = gather(hot_r, tab_r, rows, (4, 5), halo_rows)
-            lin = acc[rows, :] + pick_half(from_s, code_s[rows, :] > 0)
-            lin = lin + pick_half(from_r, code_r[rows, :] == 1)
+            lin = with_picked(acc[rows, :], from_s, from_r, rows)
             return jnp.maximum(lin, 0.0).astype(BF16)
 
         def message_of(j, hidden):
@@ -234,17 +242,12 @@
             pair = beside(hidden[0:half, :], hidden[half:tile, :])
             out = mm(pair, beside(w_o2[s, 0, :, :], w_o2[s, 1, :, :]))
             out = layer_norm(below(out[:, 0:128], out[:, 128:256]))
-            code = code_r[rows, :]
-            low = jnp.where(code == 0, out, 0.0).astype(BF16)
-            high = jnp.where(code == 1, out, 0.0).astype(BF16)
+            out = out.astype(BF16)
+            low = out * masks[0, rows, :]
+            high = out * masks[1, rows, :]
             msg2[0, rows, :] = low
             msg2[1, rows, :] = high
-            message = low.astype(F32) + high.astype(F32)
-            e[rows, :] = (e[rows, :].astype(F32) + message).astype(BF16)
-
-            @pl.when(s == LAYERS - 1)
-            def _():
-                pltpu.make_async_copy(e.at[rows, :], e_out.at[rows, :], eo_sem.at[j]).start()
+            e[rows, :] = e[rows, :] + (low + high)
 
         hidden = hidden_of(0)
         for j in range(tiles):
@@ -254,18 +257,19 @@
 
         def scatter(row_from, row_to):
             return mm(beside(*[hot_t[c, row_from:row_to, :] for c in range(edges // 128)]),
-                      beside(msg2[0, 0:edges, :], msg2[1, 0:edges, :]))
-
-        sums = scatter(512, 768).astype(BF16)
-        for k in range(4):
-            ret_buf[s, k, :, :] = sums[(k % 2) * 128 : (k % 2 + 1) * 128,
-                                       (k // 2) * 128 : (k // 2 + 1) * 128]
+                      beside(msg2[0, 0:edges, :], msg2[1, 0:edges, :])).astype(BF16)
+
+        for i in range(2):
+            sums = scatter(512 + i * 128, 640 + i * 128)
+            ret_buf[s, i, :, :] = sums[:, 0:128]
+            ret_buf[s, 2 + i, :, :] = sums[:, 128:256]
         for k in (2, 3, 0, 1):
             ret_copy(s, k).start()
 
-        owned = scatter(0, 512).astype(BF16)
-        own_buf[s, 0:512, :] = owned[:, 0:128]
-        own_buf[s, 512:1024, :] = owned[:, 128:256]
+        for i in range(4):
+            owned = scatter(i * 128, (i + 1) * 128)
+            own_buf[s, i * 128 : (i + 1) * 128, :] = owned[:, 0:128]
+            own_buf[s, 512 + i * 128 : 512 + (i + 1) * 128, :] = owned[:, 128:256]
         own_copy(s).start()
 
         for k in (0, 1, 2, 3):
@@ -301,7 +305,6 @@
         return carry
 
     lax.fori_loop(0, LAYERS, layer_step, 0)
-    x_out[...] = x[...]
 
     for s in range(LAYERS):
         for k in range(4):
@@ -309,9 +312,6 @@
             ret_copy(s, k).wait_send()
             relay_copy(s, k).wait_send()
         own_copy(s).wait_send()
-    for j in range(tiles):
-        rows = pl.ds(j * tile, tile)
-        pltpu.make_async_copy(e.at[rows, :], e_out.at[rows, :], eo_sem.at[j]).wait()
 
 
 def local(
@@ -323,16 +323,14 @@
     tile = min(512, edges)
     tiles = edges // tile
     vmem = pl.BlockSpec(memory_space=pltpu.VMEM)
-    anywhere = pl.BlockSpec(memory_space=pl.ANY)
+    hbm = pl.BlockSpec(memory_space=pltpu.HBM)
     dma = pltpu.SemaphoreType.DMA
     scratch = [
-        pltpu.VMEM((1024, 128), BF16),
-        pltpu.VMEM((edges, 128), BF16),
         pltpu.VMEM((6, edges, 128), BF16),
         pltpu.VMEM((6, edges, 128), BF16),
         pltpu.VMEM((edges // 128, 768, 128), BF16),
         pltpu.VMEM((edges, 128), I32),
-        pltpu.VMEM((edges, 128), I32),
+        pltpu.VMEM((2, edges, 128), BF16),
         pltpu.VMEM((edges, 128), F32),
         pltpu.VMEM((2, edges, 128), BF16),
         pltpu.VMEM((4, 512, 128), BF16),
@@ -353,22 +351,22 @@
         pltpu.VMEM((LAYERS, 2, 4, 128, 128), BF16),
         pltpu.VMEM((LAYERS, 1024, 128), BF16),
         pltpu.VMEM((LAYERS, 1024, 128), BF16),
-        dma, dma((tiles,)), dma((4,)), dma((4,)),
+        dma, dma((4,)), dma((4,)),
         dma((LAYERS, 4)), dma((LAYERS, 4)), dma((LAYERS, 4)), dma((LAYERS, 4)),
         dma((LAYERS, 4)), dma((LAYERS, 4)), dma((LAYERS,)), dma((LAYERS,)),
     ]
     return pl.pallas_call(
         functools.partial(kernel, doms, tile),
         out_shape=(
-            jax.ShapeDtypeStruct(node_latent.shape, BF16),
-            jax.ShapeDtypeStruct(edge_latent.shape, BF16),
+            pltpu.VMEM(node_latent.shape, BF16),
+            pltpu.VMEM(edge_latent.shape, BF16),
         ),
-        in_specs=[vmem, anywhere, vmem, vmem, pl.BlockSpec(memory_space=pltpu.SMEM)]
+        in_specs=[vmem, hbm, vmem, vmem, pl.BlockSpec(memory_space=pltpu.SMEM)]
         + [vmem] * 5,
-        out_specs=(vmem, anywhere),
+        out_specs=(vmem, vmem),
         scratch_shapes=scratch,
         compiler_params=pltpu.CompilerParams(
-            collective_id=0, has_side_effects=True, vmem_limit_bytes=60 << 20,
+            collective_id=0, has_side_effects=True, vmem_limit_bytes=65700000,
         ),
     )(
         node_latent, edge_latent,

time: 75.4 us -> 69.9 us (0.927)
  Pallas kernels: 70 us -> 66.8 us
  local copies, waits for them, and re-layouts: 3.93 us -> 1.67 us
    pallas_call x1, Pallas kernels: 70 us -> 66.8 us  [local(): pl.pallas_call(functools.partial(kernel, doms, tile), out_shape=(pltpu.VM...]
    unnamed x2, local copies, waits for them, and re-layouts: 3.93 us -> 1.67 us
where the time goes in v3:
time: 69.9 us; the launch traced here: 69.8 us
  Pallas kernels  66.8 us (96%)
  local copies, waits for them, and re-layouts  1.67 us (2%)
  between operations  1.29 us (2%)
    pallas_call x1, Pallas kernels, local(): pl.pallas_call(functools.partial(kernel, doms, tile), out_shape=(pltpu.VM...  66.8 us
    unnamed x2, local copies, waits for them, and re-layouts  1.67 us

profile of v3, /device:TPU:1, one launch (start us, length us, event | category | flops | bytes accessed | tf_op | source)
XLA Modules:
  0.0 69.8 jit_solution(2539992127416881412)
XLA Ops:
  1.3 66.8 %shard_map.113 = (bf16[1024,128]{1,0:T(8,128)(2,1)S(1)}, bf16[4096,128]{1,0:T(8,128)(2,1)S(1)}) custom-call(bf16[1024,128]{1,0:T(8,128)(2,1)} %x_in.1, bf16[4096,128]{1,0:T(8,128)(2,1)} %e_hbm.1, s32[32,128]{1,0:T(8,128)} %bitcast.9, s32[32,128]{1,0:T(8,128)} %bitcast.10, s32[1,1]{1,0:T(1,128)} %bitcast.6.cnt, s32[4,128]{1,0:T(4,128)} %bitcast.11, ...), custom_call_target="tpu_custom_call" | custom-call | tf_op jit(solution)/shard_map/pallas_call | solution.py:358
  68.1 0.7 %copy.14 = bf16[1024,128]{1,0:T(8,128)(2,1)} copy(bf16[1024,128]{1,0:T(8,128)(2,1)S(1)} %get-tuple-element.2) | data formatting | bytes 524288
  68.8 1.0 %copy.15 = bf16[4096,128]{1,0:T(8,128)(2,1)} copy(bf16[4096,128]{1,0:T(8,128)(2,1)S(1)} %get-tuple-element.3) | data formatting | bytes 2097152

commit v4 on v3

--- a/solution.py
+++ b/solution.py
@@ -56,8 +56,8 @@
     doms, tile,
     x_in, e_hbm, snd, rcv, cnt, sidx, w_in, w_out, n_in, n_out,
     x, e,
-    hot_s, hot_r, hot_t, code, masks, acc, msg2,
-    pick, pick_t, pick_hi, tab_s, tab_r,
+    hot_s, hot_r, hot_t, code, acc, msg2,
+    pick, pick_t, pick_hi, tab_s, tab_r, back_sum, own_sum, own_lin,
     w_in_t, n_in_t, w_out_full, n_out_full, w_sr_t, w_e2, w_o2,
     fwd_buf, halo, ret_buf, ret, own_buf, own_peer,
     e_sem, w_send, w_recv, fwd_send, fwd_recv, ret_send, ret_recv,
@@ -66,8 +66,8 @@
     p = lax.axis_index("dom")
     t = lax.axis_index("tp")
     peer = (p, 1 - t)
-    to = [(lax.rem(p + o + doms, doms), t) for o in OFFSETS]
-    back = [(lax.rem(p - o + doms, doms), t) for o in OFFSETS]
+    to = [(lax.rem(p + o + doms, doms), 1 - t) for o in OFFSETS]
+    back = [(lax.rem(p - o + doms, doms), 1 - t) for o in OFFSETS]
     edges = e.shape[0]
     tiles = edges // tile
     half = tile // 2
@@ -91,7 +91,7 @@
                       fwd_send.at[layer, k], fwd_recv.at[layer, k], to[k])
 
     def ret_copy(layer, k):
-        return remote(ret_buf.at[layer, k], ret.at[layer, t, k],
+        return remote(ret_buf.at[layer, k], ret.at[layer, 1 - t, k],
                       ret_send.at[layer, k], ret_recv.at[layer, k], back[k])
 
     def relay_copy(layer, k):
@@ -111,29 +111,28 @@
 
     lane = lax.broadcasted_iota(I32, (128, 128), 1)
     sub = lax.broadcasted_iota(I32, (128, 128), 0)
-    lane16 = lax.broadcasted_iota(I32, (16, 128), 1).astype(I16)
     sub16 = lax.broadcasted_iota(I32, (16, 128), 0).astype(I16)
-    lane_of = [lane16 + I16(g * 128) for g in range(6)]
+    lane_of = [lax.broadcasted_iota(I32, (16, 128), 1) + g * 128 for g in range(6)]
 
     def hot_columns(ref, groups, start, low):
         for i in range(8):
             part = low[i * 16 : (i + 1) * 16, :]
             for g in range(groups):
-                ref[g, pl.ds(start + i * 16, 16), :] = hot(part == lane_of[g])
-
-    def hot_rows(ref, c, count, low_row):
+                ref[g, pl.ds(start + i * 16, 16), :] = jnp.where(
+                    part == lane_of[g], 1.0, 0.0).astype(BF16)
+
+    def hot_rows(ref, c, row_from, row_to, low_row):
         wide = jnp.broadcast_to(low_row, (16, 128)).astype(I16)
-        for i in range(count // 16):
+        for i in range(row_from // 16, row_to // 16):
             ref[c, i * 16 : (i + 1) * 16, :] = hot(wide - I16(i * 16) == sub16)
 
     for k in range(4):
         row = sidx[pl.ds(k, 1), :]
         wide = column(row)
         rows = pl.ds(k * 128, 128)
-        low = jnp.where(wide < 0, -1, wide & 511).astype(I16)
+        low = jnp.where(wide < 0, -1, wide & 511)
         pick_hi[rows, :] = jnp.where(wide >= 512, 1, 0)
         hot_columns(pick, 4, k * 128, low)
-        hot_rows(pick_t, k, 512, jnp.where(row < 0, -1, row & 511))
 
     def fill_fwd(layer):
         table = beside(x[0:512, :], x[512:1024, :])
@@ -144,15 +143,15 @@
 
     x[...] = x_in[...]
     fill_fwd(0)
-    pl.semaphore_wait(barrier, 5)
-    for k in (2, 3, 0, 1):
-        fwd_copy(0, k).start()
-    for copy in weight_copies:
-        copy.start()
     for src, dst in [(w_in, w_in_t), (w_out, w_out_full), (n_in, n_in_t), (n_out, n_out_full)]:
         dst[:, rows64, :] = src[...]
     w_e2[...] = jnp.zeros_like(w_e2)
     w_o2[...] = jnp.zeros_like(w_o2)
+    pl.semaphore_wait(barrier, 5)
+    for k in range(4):
+        fwd_copy(0, k).start()
+    for copy in weight_copies:
+        copy.start()
 
     live = cnt[0, 0]
 
@@ -162,25 +161,26 @@
         high = jnp.where(own, row >> 9, (row >> 8) & 1)
         return low, high
 
-    def build(c, carry):
+    def build_one(c):
         start = pl.multiple_of(c * 128, 128)
         rows = pl.ds(start, 128)
         low, high = split(snd[pl.ds(c, 1), :])
         low_r, high_r = split(rcv[pl.ds(c, 1), :])
-        hot_rows(hot_t, c, 768, low_r)
+        hot_rows(hot_t, c, 512, 768, low_r)
         both = column(low + high * 1024)
         both_r = column(low_r + high_r * 1024)
-        hot_columns(hot_s, 6, start, (both & 1023).astype(I16))
-        hot_columns(hot_r, 6, start, (both_r & 1023).astype(I16))
-        high = both >> 10
-        high_r = both_r >> 10
-        code[rows, :] = high + 2 * high_r
-        place = jnp.where(sub + start < live, high_r, 2)
-        masks[0, rows, :] = jnp.where(place == 0, 1.0, 0.0).astype(BF16)
-        masks[1, rows, :] = jnp.where(place == 1, 1.0, 0.0).astype(BF16)
+        hot_columns(hot_s, 6, start, both & 1023)
+        hot_columns(hot_r, 6, start, both_r & 1023)
+        alive = sub + start < live
+        held = jnp.where(both_r >= 1024, jnp.where(alive, 6, 4), jnp.where(alive, 0, 2))
+        code[rows, :] = held + (both >> 10)
+
+    def build(i, carry):
+        for c in range(4):
+            build_one(i * 4 + c)
         return carry
 
-    lax.fori_loop(0, edges // 128, build, 0)
+    lax.fori_loop(0, edges // 512, build, 0)
 
     for copy in weight_copies:
         copy.wait()
@@ -208,7 +208,7 @@
         def with_picked(lin, from_s, from_r, rows):
             held = code[rows, :]
             lin = lin + pick_half(from_s, (held & 1) > 0)
-            return lin + pick_half(from_r, held > 1)
+            return lin + pick_half(from_r, held >= 4)
 
         owned_rows = pl.ds(0, 512)
         for j in range(tiles):
@@ -242,12 +242,9 @@
             pair = beside(hidden[0:half, :], hidden[half:tile, :])
             out = mm(pair, beside(w_o2[s, 0, :, :], w_o2[s, 1, :, :]))
             out = layer_norm(below(out[:, 0:128], out[:, 128:256]))
-            out = out.astype(BF16)
-            low = out * masks[0, rows, :]
-            high = out * masks[1, rows, :]
-            msg2[0, rows, :] = low
-            msg2[1, rows, :] = high
-            e[rows, :] = e[rows, :] + (low + high)
+            held = code[rows, :]
+            msg2[0, rows, :] = jnp.where(held < 2, out, 0.0).astype(BF16)
+            msg2[1, rows, :] = jnp.where(held >= 6, out, 0.0).astype(BF16)
 
         hidden = hidden_of(0)
         for j in range(tiles):
@@ -263,8 +260,20 @@
             sums = scatter(512 + i * 128, 640 + i * 128)
             ret_buf[s, i, :, :] = sums[:, 0:128]
             ret_buf[s, 2 + i, :, :] = sums[:, 128:256]
-        for k in (2, 3, 0, 1):
+        for k in range(4):
             ret_copy(s, k).start()
+
+        @pl.when(s == 0)
+        def _():
+            for k in range(4):
+                row = sidx[pl.ds(k, 1), :]
+                hot_rows(pick_t, k, 0, 512, jnp.where(row < 0, -1, row & 511))
+
+            def build_owned(c, carry):
+                hot_rows(hot_t, c, 0, 512, split(rcv[pl.ds(c, 1), :])[0])
+                return carry
+
+            lax.fori_loop(0, edges // 128, build_owned, 0)
 
         for i in range(4):
             owned = scatter(i * 128, (i + 1) * 128)
@@ -272,34 +281,44 @@
             own_buf[s, 512 + i * 128 : 512 + (i + 1) * 128, :] = owned[:, 128:256]
         own_copy(s).start()
 
-        for k in (0, 1, 2, 3):
+        for j in range(tiles):
+            rows = pl.ds(j * tile, tile)
+            message = msg2[0, rows, :].astype(F32) + msg2[1, rows, :].astype(F32)
+            e[rows, :] = (e[rows, :].astype(F32) + message).astype(BF16)
+
+        high = pick_hi[...] > 0
+        places = beside(*[pick_t[k, :, :] for k in range(4)])
+
+        def returned_sum(source):
+            block = below(*[ret[s, source, k, :, :] for k in range(4)]).astype(F32)
+            both = beside(jnp.where(high, 0.0, block), jnp.where(high, block, 0.0))
+            return mm(places, both.astype(BF16))
+
+        for k in range(4):
             ret_copy(s, k).wait_recv()
             relay_copy(s, k).start()
         own_copy(s).wait_recv()
-        for k in (0, 1, 2, 3):
-            relay_copy(s, k).wait_recv()
-
-        high = pick_hi[...] > 0
-        places = beside(*[pick_t[k, :, :] for k in range(4)])
-        back_sum = None
-        for source in range(2):
-            block = below(*[ret[s, source, k, :, :] for k in range(4)]).astype(F32)
-            both = beside(jnp.where(high, 0.0, block), jnp.where(high, block, 0.0)).astype(BF16)
-            part = mm(places, both)
-            back_sum = part if back_sum is None else back_sum + part
+        back_sum[...] = returned_sum(t)
         for h in range(2):
             rows = pl.ds(h * 512, 512)
-            now = x[rows, :]
-            both = own_buf[s, rows, :].astype(F32) + own_peer[s, rows, :].astype(F32)
-            total = (both + back_sum[:, h * 128 : (h + 1) * 128]).astype(BF16)
-            hidden = jnp.maximum(mm_t(beside(now, total), n_in_t[s, :, :]), 0.0).astype(BF16)
+            own_sum[rows, :] = own_buf[s, rows, :].astype(F32) + own_peer[s, rows, :].astype(F32)
+            own_lin[rows, :] = mm_t(x[rows, :], n_in_t[s, :, 0:128])
+        for k in range(4):
+            relay_copy(s, k).wait_recv()
+
+        back = back_sum[...] + returned_sum(1 - t)
+        for h in range(2):
+            rows = pl.ds(h * 512, 512)
+            total = (own_sum[rows, :] + back[:, h * 128 : (h + 1) * 128]).astype(BF16)
+            lin = own_lin[rows, :] + mm_t(total, n_in_t[s, :, 128:256])
+            hidden = jnp.maximum(lin, 0.0).astype(BF16)
             update = layer_norm(mm(hidden, n_out_full[s, :, :]))
-            x[rows, :] = (now.astype(F32) + update).astype(BF16)
+            x[rows, :] = (x[rows, :].astype(F32) + update).astype(BF16)
 
         @pl.when(s < LAYERS - 1)
         def _():
             fill_fwd(s + 1)
-            for k in (2, 3, 0, 1):
+            for k in range(4):
                 fwd_copy(s + 1, k).start()
 
         return carry
@@ -330,7 +349,6 @@
         pltpu.VMEM((6, edges, 128), BF16),
         pltpu.VMEM((edges // 128, 768, 128), BF16),
         pltpu.VMEM((edges, 128), I32),
-        pltpu.VMEM((2, edges, 128), BF16),
         pltpu.VMEM((edges, 128), F32),
         pltpu.VMEM((2, edges, 128), BF16),
         pltpu.VMEM((4, 512, 128), BF16),
@@ -338,6 +356,9 @@
         pltpu.VMEM((512, 128), I32),
         pltpu.VMEM((2, 768, 128), BF16),
         pltpu.VMEM((2, 768, 128), BF16),
+        pltpu.VMEM((512, 256), F32),
+        pltpu.VMEM((1024, 128), F32),
+        pltpu.VMEM((1024, 128), F32),
         pltpu.VMEM((LAYERS, 128, 384), BF16),
         pltpu.VMEM((LAYERS, 128, 256), BF16),
         pltpu.VMEM((LAYERS, 128, 128), BF16),

time: 69.9 us -> 65.8 us (0.941)
  Pallas kernels: 66.8 us -> 62.7 us
    pallas_call x1, Pallas kernels: 66.8 us -> 62.7 us  [local(): pl.pallas_call(functools.partial(kernel, doms, tile), out_shape=(pltpu.VM...]
where the time goes in v4:
time: 65.8 us; the launch traced here: 65.7 us
  Pallas kernels  62.7 us (95%)
  local copies, waits for them, and re-layouts  1.67 us (3%)
  between operations  1.29 us (2%)
    pallas_call x1, Pallas kernels, local(): pl.pallas_call(functools.partial(kernel, doms, tile), out_shape=(pltpu.VM...  62.7 us
    unnamed x2, local copies, waits for them, and re-layouts  1.67 us

profile of v4, /device:TPU:1, one launch (start us, length us, event | category | flops | bytes accessed | tf_op | source)
XLA Modules:
  0.0 65.7 jit_solution(16588320011849283460)
XLA Ops:
  1.3 62.7 %shard_map.113 = (bf16[1024,128]{1,0:T(8,128)(2,1)S(1)}, bf16[4096,128]{1,0:T(8,128)(2,1)S(1)}) custom-call(bf16[1024,128]{1,0:T(8,128)(2,1)} %x_in.1, bf16[4096,128]{1,0:T(8,128)(2,1)} %e_hbm.1, s32[32,128]{1,0:T(8,128)} %bitcast.9, s32[32,128]{1,0:T(8,128)} %bitcast.10, s32[1,1]{1,0:T(1,128)} %bitcast.6.cnt, s32[4,128]{1,0:T(4,128)} %bitcast.11, ...), custom_call_target="tpu_custom_call" | custom-call | tf_op jit(solution)/shard_map/pallas_call | solution.py:379
  64.0 0.7 %copy.14 = bf16[1024,128]{1,0:T(8,128)(2,1)} copy(bf16[1024,128]{1,0:T(8,128)(2,1)S(1)} %get-tuple-element.2) | data formatting | bytes 524288
  64.7 1.0 %copy.15 = bf16[4096,128]{1,0:T(8,128)(2,1)} copy(bf16[4096,128]{1,0:T(8,128)(2,1)S(1)} %get-tuple-element.3) | data formatting | bytes 2097152

commit v5 on v4

--- a/solution.py
+++ b/solution.py
@@ -54,13 +54,14 @@
 
 def kernel(
     doms, tile,
-    x_in, e_hbm, snd, rcv, cnt, sidx, w_in, w_out, n_in, n_out,
+    x_hbm, e_hbm, snd_hbm, rcv_hbm, cnt_hbm, sidx_hbm, w_in_hbm, w_out_hbm, n_in_hbm, n_out_hbm,
     x, e,
+    snd, rcv, cnt, sidx, w_in, w_out, n_in, n_out,
     hot_s, hot_r, hot_t, code, acc, msg2,
     pick, pick_t, pick_hi, tab_s, tab_r, back_sum, own_sum, own_lin,
     w_in_t, n_in_t, w_out_full, n_out_full, w_sr_t, w_e2, w_o2,
     fwd_buf, halo, ret_buf, ret, own_buf, own_peer,
-    e_sem, w_send, w_recv, fwd_send, fwd_recv, ret_send, ret_recv,
+    in_sem, w_send, w_recv, fwd_send, fwd_recv, ret_send, ret_recv,
     rel_send, rel_recv, own_send, own_recv,
 ):
     p = lax.axis_index("dom")
@@ -77,8 +78,15 @@
     for other in to + [peer]:
         pl.semaphore_signal(barrier, inc=1, device_id=other, device_id_type=MESH)
 
-    load_e = pltpu.make_async_copy(e_hbm, e, e_sem)
-    load_e.start()
+    loads = [
+        pltpu.make_async_copy(src, dst, in_sem.at[i])
+        for i, (src, dst) in enumerate([
+            (sidx_hbm, sidx), (x_hbm, x), (w_in_hbm, w_in), (w_out_hbm, w_out),
+            (n_in_hbm, n_in), (n_out_hbm, n_out), (snd_hbm, snd), (rcv_hbm, rcv),
+            (cnt_hbm, cnt), (e_hbm, e)])
+    ]
+    for copy in loads:
+        copy.start()
 
     def remote(src, dst, send, recv, device):
         return pltpu.make_async_remote_copy(
@@ -126,6 +134,7 @@
         for i in range(row_from // 16, row_to // 16):
             ref[c, i * 16 : (i + 1) * 16, :] = hot(wide - I16(i * 16) == sub16)
 
+    loads[0].wait()
     for k in range(4):
         row = sidx[pl.ds(k, 1), :]
         wide = column(row)
@@ -136,13 +145,15 @@
 
     def fill_fwd(layer):
         table = beside(x[0:512, :], x[512:1024, :])
-        both = mm(beside(*[pick[g, :, :] for g in range(4)]), table)
-        picked = pick_half(both, pick_hi[...] > 0).astype(BF16)
-        for k in range(4):
-            fwd_buf[layer, k, :, :] = picked[k * 128 : (k + 1) * 128, :]
-
-    x[...] = x_in[...]
+        for h in range(4):
+            rows = pl.ds(h * 128, 128)
+            both = mm(beside(*[pick[g, rows, :] for g in range(4)]), table)
+            fwd_buf[layer, h, :, :] = pick_half(both, pick_hi[rows, :] > 0).astype(BF16)
+
+    loads[1].wait()
     fill_fwd(0)
+    for copy in loads[2:6]:
+        copy.wait()
     for src, dst in [(w_in, w_in_t), (w_out, w_out_full), (n_in, n_in_t), (n_out, n_out_full)]:
         dst[:, rows64, :] = src[...]
     w_e2[...] = jnp.zeros_like(w_e2)
@@ -153,6 +164,8 @@
     for copy in weight_copies:
         copy.start()
 
+    for copy in loads[6:]:
+        copy.wait()
     live = cnt[0, 0]
 
     def split(row):
@@ -162,7 +175,7 @@
         return low, high
 
     def build_one(c):
-        start = pl.multiple_of(c * 128, 128)
+        start = c * 128
         rows = pl.ds(start, 128)
         low, high = split(snd[pl.ds(c, 1), :])
         low_r, high_r = split(rcv[pl.ds(c, 1), :])
@@ -175,16 +188,11 @@
         held = jnp.where(both_r >= 1024, jnp.where(alive, 6, 4), jnp.where(alive, 0, 2))
         code[rows, :] = held + (both >> 10)
 
-    def build(i, carry):
-        for c in range(4):
-            build_one(i * 4 + c)
-        return carry
-
-    lax.fori_loop(0, edges // 512, build, 0)
-
-    for copy in weight_copies:
-        copy.wait()
-    for s in range(LAYERS):
+    def build_tile(j):
+        for c in range(chunks):
+            build_one(j * chunks + c)
+
+    def lay_out_weights(s):
         full = jnp.transpose(w_in_t[s, :, 0:128].astype(F32)).astype(BF16)
         w_e2[s, 0, 0:128, :] = full
         w_e2[s, 1, 128:256, :] = full
@@ -193,33 +201,44 @@
         full = w_out_full[s, :, :]
         w_o2[s, 0, 0:128, :] = full
         w_o2[s, 1, 128:256, :] = full
-    load_e.wait()
-
-    def layer_step(s, carry):
+
+    def project_owned(s):
         for h in range(2):
             proj = mm_t(x[h * 512 : (h + 1) * 512, :], w_sr_t[s, :, :]).astype(BF16)
             tab_s[h, 0:512, :] = proj[:, 0:128]
             tab_r[h, 0:512, :] = proj[:, 128:256]
 
-        def gather(hots, tab, rows, groups, table_rows):
-            return mm(beside(*[hots[g, rows, :] for g in groups]),
-                      beside(tab[0, table_rows, :], tab[1, table_rows, :]))
-
-        def with_picked(lin, from_s, from_r, rows):
-            held = code[rows, :]
-            lin = lin + pick_half(from_s, (held & 1) > 0)
-            return lin + pick_half(from_r, held >= 4)
-
+    def gather(hots, tab, rows, groups, table_rows):
+        return mm(beside(*[hots[g, rows, :] for g in groups]),
+                  beside(tab[0, table_rows, :], tab[1, table_rows, :]))
+
+    def with_picked(lin, from_s, from_r, rows):
+        held = code[rows, :]
+        lin = lin + pick_half(from_s, (held & 1) > 0)
+        return lin + pick_half(from_r, held >= 4)
+
+    def owned_part(s, j):
+        rows = pl.ds(j * tile, tile)
         owned_rows = pl.ds(0, 512)
-        for j in range(tiles):
-            rows = pl.ds(j * tile, tile)
-            pair = beside(e[pl.ds(j * tile, half), :], e[pl.ds(j * tile + half, half), :])
-            lin = mm(pair, beside(w_e2[s, 0, :, :], w_e2[s, 1, :, :]))
-            lin = below(lin[:, 0:128], lin[:, 128:256])
-            from_s = gather(hot_s, tab_s, rows, range(4), owned_rows)
-            from_r = gather(hot_r, tab_r, rows, range(4), owned_rows)
-            acc[rows, :] = with_picked(lin, from_s, from_r, rows)
-
+        pair = beside(e[pl.ds(j * tile, half), :], e[pl.ds(j * tile + half, half), :])
+        lin = mm(pair, beside(w_e2[s, 0, :, :], w_e2[s, 1, :, :]))
+        lin = below(lin[:, 0:128], lin[:, 128:256])
+        from_s = gather(hot_s, tab_s, rows, range(4), owned_rows)
+        from_r = gather(hot_r, tab_r, rows, range(4), owned_rows)
+        acc[rows, :] = with_picked(lin, from_s, from_r, rows)
+
+    build_tile(0)
+    build_tile(1)
+    for copy in weight_copies:
+        copy.wait()
+    lay_out_weights(0)
+    project_owned(0)
+    for j in range(tiles):
+        if j + 2 < tiles:
+            build_tile(j + 2)
+        owned_part(0, j)
+
+    def layer_step(s, carry):
         for k in range(4):
             fwd_copy(s, k).wait_recv()
         for h in range(2):
@@ -274,6 +293,8 @@
                 return carry
 
             lax.fori_loop(0, edges // 128, build_owned, 0)
+            for layer in range(1, LAYERS):
+                lay_out_weights(layer)
 
         for i in range(4):
             owned = scatter(i * 128, (i + 1) * 128)
@@ -286,18 +307,25 @@
             message = msg2[0, rows, :].astype(F32) + msg2[1, rows, :].astype(F32)
             e[rows, :] = (e[rows, :].astype(F32) + message).astype(BF16)
 
+        for k in range(4):
+            fwd_copy(s, k).wait_send()
+
         high = pick_hi[...] > 0
         places = beside(*[pick_t[k, :, :] for k in range(4)])
 
         def returned_sum(source):
             block = below(*[ret[s, source, k, :, :] for k in range(4)]).astype(F32)
             both = beside(jnp.where(high, 0.0, block), jnp.where(high, block, 0.0))
-            return mm(places, both.astype(BF16))
+            both = both.astype(BF16)
+            return below(mm(places[0:256, :], both), mm(places[256:512, :], both))
 
         for k in range(4):
             ret_copy(s, k).wait_recv()
             relay_copy(s, k).start()
         own_copy(s).wait_recv()
+        for k in range(4):
+            ret_copy(s, k).wait_send()
+        own_copy(s).wait_send()
         back_sum[...] = returned_sum(t)
         for h in range(2):
             rows = pl.ds(h * 512, 512)
@@ -321,16 +349,17 @@
             for k in range(4):
                 fwd_copy(s + 1, k).start()
 
+        @pl.when(s < LAYERS - 1)
+        def _():
+            project_owned(s + 1)
+            for j in range(tiles):
+                owned_part(s + 1, j)
+
+        for k in range(4):
+            relay_copy(s, k).wait_send()
         return carry
 
     lax.fori_loop(0, LAYERS, layer_step, 0)
-
-    for s in range(LAYERS):
-        for k in range(4):
-            fwd_copy(s, k).wait_send()
-            ret_copy(s, k).wait_send()
-            relay_copy(s, k).wait_send()
-        own_copy(s).wait_send()
 
 
 def local(
@@ -344,7 +373,16 @@
     vmem = pl.BlockSpec(memory_space=pltpu.VMEM)
     hbm = pl.BlockSpec(memory_space=pltpu.HBM)
     dma = pltpu.SemaphoreType.DMA
+    packed = (edges // 128, 128)
     scratch = [
+        pltpu.VMEM(packed, I32),
+        pltpu.VMEM(packed, I32),
+        pltpu.SMEM((1, 1), I32),
+        pltpu.VMEM((4, 128), I32),
+        pltpu.VMEM((LAYERS, 64, 384), BF16),
+        pltpu.VMEM((LAYERS, 64, 128), BF16),
+        pltpu.VMEM((LAYERS, 64, 256), BF16),
+        pltpu.VMEM((LAYERS, 64, 128), BF16),
         pltpu.VMEM((6, edges, 128), BF16),
         pltpu.VMEM((6, edges, 128), BF16),
         pltpu.VMEM((edges // 128, 768, 128), BF16),
@@ -372,7 +410,7 @@
         pltpu.VMEM((LAYERS, 2, 4, 128, 128), BF16),
         pltpu.VMEM((LAYERS, 1024, 128), BF16),
         pltpu.VMEM((LAYERS, 1024, 128), BF16),
-        dma, dma((4,)), dma((4,)),
+        dma((10,)), dma((4,)), dma((4,)),
         dma((LAYERS, 4)), dma((LAYERS, 4)), dma((LAYERS, 4)), dma((LAYERS, 4)),
         dma((LAYERS, 4)), dma((LAYERS, 4)), dma((LAYERS,)), dma((LAYERS,)),
     ]
@@ -382,8 +420,7 @@
             pltpu.VMEM(node_latent.shape, BF16),
             pltpu.VMEM(edge_latent.shape, BF16),
         ),
-        in_specs=[vmem, hbm, vmem, vmem, pl.BlockSpec(memory_space=pltpu.SMEM)]
-        + [vmem] * 5,
+        in_specs=[hbm] * 10,
         out_specs=(vmem, vmem),
         scratch_shapes=scratch,
         compiler_params=pltpu.CompilerParams(

time: 65.8 us -> 64.5 us (0.980)
  Pallas kernels: 62.7 us -> 61.4 us
    pallas_call x1, Pallas kernels: 62.7 us -> 61.4 us  [local(): pl.pallas_call(functools.partial(kernel, doms, tile), out_shape=(pltpu.VM...]
where the time goes in v5:
time: 64.5 us; the launch traced here: 64.4 us
  Pallas kernels  61.4 us (95%)
  local copies, waits for them, and re-layouts  1.67 us (3%)
  between operations  1.29 us (2%)
    pallas_call x1, Pallas kernels, local(): pl.pallas_call(functools.partial(kernel, doms, tile), out_shape=(pltpu.VM...  61.4 us
    unnamed x2, local copies, waits for them, and re-layouts  1.67 us

profile of v5, /device:TPU:1, one launch (start us, length us, event | category | flops | bytes accessed | tf_op | source)
XLA Modules:
  0.0 64.4 jit_solution(2802916405292899503)
XLA Ops:
  1.3 61.4 %shard_map.113 = (bf16[1024,128]{1,0:T(8,128)(2,1)S(1)}, bf16[4096,128]{1,0:T(8,128)(2,1)S(1)}) custom-call(bf16[1024,128]{1,0:T(8,128)(2,1)} %x_hbm.1, bf16[4096,128]{1,0:T(8,128)(2,1)} %e_hbm.1, s32[32,128]{1,0:T(8,128)} %bitcast.9, s32[32,128]{1,0:T(8,128)} %bitcast.10, s32[1,1]{1,0:T(1,128)} %bitcast.6.cnt_hbm, s32[4,128]{1,0:T(4,128)} %bitcast.11, ...), custom_call_target="tpu_custom_call" | custom-call | tf_op jit(solution)/shard_map/pallas_call | solution.py:417
  62.7 0.7 %copy.14 = bf16[1024,128]{1,0:T(8,128)(2,1)} copy(bf16[1024,128]{1,0:T(8,128)(2,1)S(1)} %get-tuple-element.2) | data formatting | bytes 524288
  63.4 1.0 %copy.15 = bf16[4096,128]{1,0:T(8,128)(2,1)} copy(bf16[4096,128]{1,0:T(8,128)(2,1)S(1)} %get-tuple-element.3) | data formatting | bytes 2097152

commit v6 on v5

--- a/solution.py
+++ b/solution.py
@@ -33,11 +33,14 @@
     return jnp.concatenate(parts, axis=0)
 
 
-def layer_norm(values):
-    centre = jnp.mean(values, axis=-1, keepdims=True)
-    centred = values - centre
-    spread = jnp.mean(centred * centred, axis=-1, keepdims=True)
-    return centred * lax.rsqrt(spread + NORM_FLOOR)
+def norm_centred(values):
+    spread = jnp.sum(values * values, axis=-1, keepdims=True) * (1.0 / 128.0)
+    return values * lax.rsqrt(spread + NORM_FLOOR)
+
+
+def centred(weights):
+    wide = weights.astype(F32)
+    return (wide - jnp.mean(wide, axis=-1, keepdims=True)).astype(BF16)
 
 
 def hot(match):
@@ -59,10 +62,9 @@
     snd, rcv, cnt, sidx, w_in, w_out, n_in, n_out,
     hot_s, hot_r, hot_t, code, acc, msg2,
     pick, pick_t, pick_hi, tab_s, tab_r, back_sum, own_sum, own_lin,
-    w_in_t, n_in_t, w_out_full, n_out_full, w_sr_t, w_e2, w_o2,
+    w_in_t, n_in_t, w_out_full, n_out_full, n_out_mid, w_sr_t, w_e2, w_o2,
     fwd_buf, halo, ret_buf, ret, own_buf, own_peer,
-    in_sem, w_send, w_recv, fwd_send, fwd_recv, ret_send, ret_recv,
-    rel_send, rel_recv, own_send, own_recv,
+    in_sem, send_sem, w_recv, fwd_recv, ret_recv, rel_recv, own_recv,
 ):
     p = lax.axis_index("dom")
     t = lax.axis_index("tp")
@@ -94,25 +96,25 @@
             device_id=device, device_id_type=MESH,
         )
 
-    def fwd_copy(layer, k):
-        return remote(fwd_buf.at[layer, k], halo.at[layer, k],
-                      fwd_send.at[layer, k], fwd_recv.at[layer, k], to[k])
-
-    def ret_copy(layer, k):
-        return remote(ret_buf.at[layer, k], ret.at[layer, 1 - t, k],
-                      ret_send.at[layer, k], ret_recv.at[layer, k], back[k])
-
-    def relay_copy(layer, k):
-        return remote(ret.at[layer, t, k], ret.at[layer, t, k],
-                      rel_send.at[layer, k], rel_recv.at[layer, k], peer)
+    def fwd_copy(layer, *k):
+        return remote(fwd_buf.at[(layer, *k)], halo.at[(layer, *k)],
+                      send_sem.at[0], fwd_recv.at[layer], to[k[0] if k else 0])
+
+    def ret_copy(layer, *k):
+        return remote(ret_buf.at[(layer, *k)], ret.at[(layer, 1 - t, *k)],
+                      send_sem.at[1], ret_recv.at[layer, k[0] if k else 0], back[k[0] if k else 0])
+
+    def relay_copy(layer, *k):
+        return remote(ret.at[(layer, t, *k)], ret.at[(layer, t, *k)],
+                      send_sem.at[2], rel_recv.at[layer], peer)
 
     def own_copy(layer):
         return remote(own_buf.at[layer], own_peer.at[layer],
-                      own_send.at[layer], own_recv.at[layer], peer)
+                      send_sem.at[3], own_recv.at[layer], peer)
 
     rows64 = pl.ds(pl.multiple_of(t * 64, 64), 64)
     weight_copies = [
-        remote(src, dst.at[:, rows64, :], w_send.at[i], w_recv.at[i], peer)
+        remote(src, dst.at[:, rows64, :], in_sem.at[2 + i], w_recv.at[i], peer)
         for i, (src, dst) in enumerate(
             [(w_in, w_in_t), (w_out, w_out_full), (n_in, n_in_t), (n_out, n_out_full)])
     ]
@@ -198,7 +200,7 @@
         w_e2[s, 1, 128:256, :] = full
         w_sr_t[s, 0:128, :] = w_in_t[s, :, 128:256]
         w_sr_t[s, 128:256, :] = w_in_t[s, :, 256:384]
-        full = w_out_full[s, :, :]
+        full = centred(w_out_full[s, :, :])
         w_o2[s, 0, 0:128, :] = full
         w_o2[s, 1, 128:256, :] = full
 
@@ -239,8 +241,7 @@
         owned_part(0, j)
 
     def layer_step(s, carry):
-        for k in range(4):
-            fwd_copy(s, k).wait_recv()
+        fwd_copy(s).wait_recv()
         for h in range(2):
             held = below(halo[s, 2 * h, :, :], halo[s, 2 * h + 1, :, :])
             proj = mm_t(held, w_sr_t[s, :, :]).astype(BF16)
@@ -260,7 +261,7 @@
             rows = pl.ds(j * tile, tile)
             pair = beside(hidden[0:half, :], hidden[half:tile, :])
             out = mm(pair, beside(w_o2[s, 0, :, :], w_o2[s, 1, :, :]))
-            out = layer_norm(below(out[:, 0:128], out[:, 128:256]))
+            out = norm_centred(below(out[:, 0:128], out[:, 128:256]))
             held = code[rows, :]
             msg2[0, rows, :] = jnp.where(held < 2, out, 0.0).astype(BF16)
             msg2[1, rows, :] = jnp.where(held >= 6, out, 0.0).astype(BF16)
@@ -293,8 +294,10 @@
                 return carry
 
             lax.fori_loop(0, edges // 128, build_owned, 0)
-            for layer in range(1, LAYERS):
-                lay_out_weights(layer)
+            for layer in range(LAYERS):
+                n_out_mid[layer, :, :] = centred(n_out_full[layer, :, :])
+                if layer > 0:
+                    lay_out_weights(layer)
 
         for i in range(4):
             owned = scatter(i * 128, (i + 1) * 128)
@@ -307,8 +310,7 @@
             message = msg2[0, rows, :].astype(F32) + msg2[1, rows, :].astype(F32)
             e[rows, :] = (e[rows, :].astype(F32) + message).astype(BF16)
 
-        for k in range(4):
-            fwd_copy(s, k).wait_send()
+        fwd_copy(s).wait_send()
 
         high = pick_hi[...] > 0
         places = beside(*[pick_t[k, :, :] for k in range(4)])
@@ -323,16 +325,14 @@
             ret_copy(s, k).wait_recv()
             relay_copy(s, k).start()
         own_copy(s).wait_recv()
-        for k in range(4):
-            ret_copy(s, k).wait_send()
+        ret_copy(s).wait_send()
         own_copy(s).wait_send()
         back_sum[...] = returned_sum(t)
         for h in range(2):
             rows = pl.ds(h * 512, 512)
             own_sum[rows, :] = own_buf[s, rows, :].astype(F32) + own_peer[s, rows, :].astype(F32)
             own_lin[rows, :] = mm_t(x[rows, :], n_in_t[s, :, 0:128])
-        for k in range(4):
-            relay_copy(s, k).wait_recv()
+        relay_copy(s).wait_recv()
 
         back = back_sum[...] + returned_sum(1 - t)
         for h in range(2):
@@ -340,7 +340,7 @@
             total = (own_sum[rows, :] + back[:, h * 128 : (h + 1) * 128]).astype(BF16)
             lin = own_lin[rows, :] + mm_t(total, n_in_t[s, :, 128:256])
             hidden = jnp.maximum(lin, 0.0).astype(BF16)
-            update = layer_norm(mm(hidden, n_out_full[s, :, :]))
+            update = norm_centred(mm(hidden, n_out_mid[s, :, :]))
             x[rows, :] = (x[rows, :].astype(F32) + update).astype(BF16)
 
         @pl.when(s < LAYERS - 1)
@@ -355,11 +355,21 @@
             for j in range(tiles):
                 owned_part(s + 1, j)
 
-        for k in range(4):
-            relay_copy(s, k).wait_send()
+        relay_copy(s).wait_send()
         return carry
 
     lax.fori_loop(0, LAYERS, layer_step, 0)
+
+
+def copy_out(x, e, x_out, e_out, sem):
+    copies = [
+        pltpu.make_async_copy(e, e_out, sem.at[0]),
+        pltpu.make_async_copy(x, x_out, sem.at[1]),
+    ]
+    for copy in copies:
+        copy.start()
+    for copy in copies:
+        copy.wait()
 
 
 def local(
@@ -401,6 +411,7 @@
         pltpu.VMEM((LAYERS, 128, 256), BF16),
         pltpu.VMEM((LAYERS, 128, 128), BF16),
         pltpu.VMEM((LAYERS, 128, 128), BF16),
+        pltpu.VMEM((LAYERS, 128, 128), BF16),
         pltpu.VMEM((LAYERS, 256, 128), BF16),
         pltpu.VMEM((LAYERS, 2, 256, 128), BF16),
         pltpu.VMEM((LAYERS, 2, 256, 128), BF16),
@@ -410,11 +421,10 @@
         pltpu.VMEM((LAYERS, 2, 4, 128, 128), BF16),
         pltpu.VMEM((LAYERS, 1024, 128), BF16),
         pltpu.VMEM((LAYERS, 1024, 128), BF16),
-        dma((10,)), dma((4,)), dma((4,)),
-        dma((LAYERS, 4)), dma((LAYERS, 4)), dma((LAYERS, 4)), dma((LAYERS, 4)),
-        dma((LAYERS, 4)), dma((LAYERS, 4)), dma((LAYERS,)), dma((LAYERS,)),
+        dma((10,)), dma((4,)), dma((4,)), dma((LAYERS,)), dma((LAYERS, 4)),
+        dma((LAYERS,)), dma((LAYERS,)),
     ]
-    return pl.pallas_call(
+    nodes, edges_now = pl.pallas_call(
         functools.partial(kernel, doms, tile),
         out_shape=(
             pltpu.VMEM(node_latent.shape, BF16),
@@ -432,6 +442,18 @@
         edge_count.reshape(1, 1), send_index.reshape(4, 128),
         jnp.swapaxes(edge_in, 1, 2), edge_out, jnp.swapaxes(node_in, 1, 2), node_out,
     )
+    anywhere = pl.BlockSpec(memory_space=pl.ANY)
+    return pl.pallas_call(
+        copy_out,
+        out_shape=(
+            jax.ShapeDtypeStruct(node_latent.shape, BF16),
+            jax.ShapeDtypeStruct(edge_latent.shape, BF16),
+        ),
+        in_specs=[anywhere, anywhere],
+        out_specs=(anywhere, anywhere),
+        scratch_shapes=[dma((2,))],
+        compiler_params=pltpu.CompilerParams(vmem_limit_bytes=8 << 20),
+    )(nodes, edges_now)
 
 
 def solution(mesh):

time: 64.5 us -> 63.1 us (0.978)
  local copies, waits for them, and re-layouts: 1.67 us -> 0 us
    unnamed x2 -> x0, local copies, waits for them, and re-layouts: 1.67 us -> none
    pallas_call x0 -> x1, Pallas kernels: none -> 1.07 us  [local(): pl.pallas_call(copy_out, out_shape=(jax.ShapeDtypeStruct(node_latent.shap...]
    pallas_call x1, Pallas kernels: 61.4 us -> 60.5 us  [local(): pl.pallas_call(functools.partial(kernel, doms, tile), out_shape=(pltpu.VM...]
where the time goes in v6:
time: 63.1 us; the launch traced here: 63 us
  Pallas kernels  61.6 us (98%)
  between operations  1.45 us (2%)
    pallas_call x1, Pallas kernels, local(): pl.pallas_call(functools.partial(kernel, doms, tile), out_shape=(pltpu.VM...  60.5 us

profile of v6, /device:TPU:1, one launch (start us, length us, event | category | flops | bytes accessed | tf_op | source)
XLA Modules:
  0.0 63.0 jit_solution(12220948369940580768)
XLA Ops:
  1.3 60.5 %shard_map.113 = (bf16[1024,128]{1,0:T(8,128)(2,1)S(1)}, bf16[4096,128]{1,0:T(8,128)(2,1)S(1)}) custom-call(bf16[1024,128]{1,0:T(8,128)(2,1)} %x_hbm.1, bf16[4096,128]{1,0:T(8,128)(2,1)} %e_hbm.1, s32[32,128]{1,0:T(8,128)} %bitcast.9, s32[32,128]{1,0:T(8,128)} %bitcast.10, s32[1,1]{1,0:T(1,128)} %bitcast.6.cnt_hbm, s32[4,128]{1,0:T(4,128)} %bitcast.11, ...), custom_call_target="tpu_custom_call" | custom-call | tf_op jit(solution)/shard_map/pallas_call | solution.py:427
  61.8 1.1 %shard_map.114 = (bf16[1024,128]{1,0:T(8,128)(2,1)}, bf16[4096,128]{1,0:T(8,128)(2,1)}) custom-call(bf16[1024,128]{1,0:T(8,128)(2,1)S(1)} %get-tuple-element.4.x, bf16[4096,128]{1,0:T(8,128)(2,1)S(1)} %get-tuple-element.5.e), custom_call_target="tpu_custom_call" | custom-call | tf_op jit(solution)/shard_map/pallas_call | solution.py:446

commit v7 on v6

--- a/solution.py
+++ b/solution.py
@@ -59,9 +59,10 @@
     doms, tile,
     x_hbm, e_hbm, snd_hbm, rcv_hbm, cnt_hbm, sidx_hbm, w_in_hbm, w_out_hbm, n_in_hbm, n_out_hbm,
     x, e,
-    snd, rcv, cnt, sidx, w_in, w_out, n_in, n_out,
+    snd, rcv, codes, cnt, sidx, w_in, w_out, n_in, n_out,
     hot_s, hot_r, hot_t, code, acc, msg2,
     pick, pick_t, pick_hi, tab_s, tab_r, back_sum, own_sum, own_lin,
+    same, sent_x, sent_lin, sent_sum, sent_back,
     w_in_t, n_in_t, w_out_full, n_out_full, n_out_mid, w_sr_t, w_e2, w_o2,
     fwd_buf, halo, ret_buf, ret, own_buf, own_peer,
     in_sem, send_sem, w_recv, fwd_recv, ret_recv, rel_recv, own_recv,
@@ -136,6 +137,9 @@
         for i in range(row_from // 16, row_to // 16):
             ref[c, i * 16 : (i + 1) * 16, :] = hot(wide - I16(i * 16) == sub16)
 
+    w_e2[...] = jnp.zeros_like(w_e2)
+    w_o2[...] = jnp.zeros_like(w_o2)
+
     loads[0].wait()
     for k in range(4):
         row = sidx[pl.ds(k, 1), :]
@@ -145,21 +149,25 @@
         pick_hi[rows, :] = jnp.where(wide >= 512, 1, 0)
         hot_columns(pick, 4, k * 128, low)
 
-    def fill_fwd(layer):
-        table = beside(x[0:512, :], x[512:1024, :])
-        for h in range(4):
-            rows = pl.ds(h * 128, 128)
+    def picked(top, bottom):
+        table = beside(top, bottom)
+        parts = []
+        for h in range(2):
+            rows = pl.ds(h * 256, 256)
             both = mm(beside(*[pick[g, rows, :] for g in range(4)]), table)
-            fwd_buf[layer, h, :, :] = pick_half(both, pick_hi[rows, :] > 0).astype(BF16)
+            parts.append(pick_half(both, pick_hi[rows, :] > 0))
+        return below(*parts)
+
+    def fill_fwd(layer, rows):
+        for k in range(4):
+            fwd_buf[layer, k, :, :] = rows[k * 128 : (k + 1) * 128, :]
 
     loads[1].wait()
-    fill_fwd(0)
+    fill_fwd(0, picked(x[0:512, :], x[512:1024, :]).astype(BF16))
     for copy in loads[2:6]:
         copy.wait()
     for src, dst in [(w_in, w_in_t), (w_out, w_out_full), (n_in, n_in_t), (n_out, n_out_full)]:
         dst[:, rows64, :] = src[...]
-    w_e2[...] = jnp.zeros_like(w_e2)
-    w_o2[...] = jnp.zeros_like(w_o2)
     pl.semaphore_wait(barrier, 5)
     for k in range(4):
         fwd_copy(0, k).start()
@@ -176,19 +184,23 @@
         high = jnp.where(own, row >> 9, (row >> 8) & 1)
         return low, high
 
+    low, high_s = split(snd[...])
+    snd[...] = low
+    low, high = split(rcv[...])
+    rcv[...] = low
+    slot = (lax.broadcasted_iota(I32, snd.shape, 0) * 128
+            + lax.broadcasted_iota(I32, snd.shape, 1))
+    alive = slot < live
+    codes[...] = high_s + jnp.where(
+        high > 0, jnp.where(alive, 6, 4), jnp.where(alive, 0, 2))
+
     def build_one(c):
-        start = c * 128
-        rows = pl.ds(start, 128)
-        low, high = split(snd[pl.ds(c, 1), :])
-        low_r, high_r = split(rcv[pl.ds(c, 1), :])
-        hot_rows(hot_t, c, 512, 768, low_r)
-        both = column(low + high * 1024)
-        both_r = column(low_r + high_r * 1024)
-        hot_columns(hot_s, 6, start, both & 1023)
-        hot_columns(hot_r, 6, start, both_r & 1023)
-        alive = sub + start < live
-        held = jnp.where(both_r >= 1024, jnp.where(alive, 6, 4), jnp.where(alive, 0, 2))
-        code[rows, :] = held + (both >> 10)
+        rows = pl.ds(c * 128, 128)
+        row = rcv[pl.ds(c, 1), :]
+        hot_rows(hot_t, c, 512, 768, row)
+        hot_columns(hot_s, 6, c * 128, column(snd[pl.ds(c, 1), :]))
+        hot_columns(hot_r, 6, c * 128, column(row))
+        code[rows, :] = column(codes[pl.ds(c, 1), :])
 
     def build_tile(j):
         for c in range(chunks):
@@ -288,9 +300,17 @@
             for k in range(4):
                 row = sidx[pl.ds(k, 1), :]
                 hot_rows(pick_t, k, 0, 512, jnp.where(row < 0, -1, row & 511))
+                wide = column(row)
+                wide = jnp.where(wide < 0, -2, wide)
+                for i in range(8):
+                    part = wide[i * 16 : (i + 1) * 16, :]
+                    for g in range(4):
+                        other = jnp.broadcast_to(sidx[pl.ds(g, 1), :], (16, 128))
+                        same[g, pl.ds(k * 128 + i * 16, 16), :] = jnp.where(
+                            part == other, 1.0, 0.0).astype(BF16)
 
             def build_owned(c, carry):
-                hot_rows(hot_t, c, 0, 512, split(rcv[pl.ds(c, 1), :])[0])
+                hot_rows(hot_t, c, 0, 512, rcv[pl.ds(c, 1), :])
                 return carry
 
             lax.fori_loop(0, edges // 128, build_owned, 0)
@@ -321,18 +341,44 @@
             both = both.astype(BF16)
             return below(mm(places[0:256, :], both), mm(places[256:512, :], both))
 
-        for k in range(4):
-            ret_copy(s, k).wait_recv()
-            relay_copy(s, k).start()
+        def returned_sent(source):
+            block = below(*[ret[s, source, k, :, :] for k in range(4)])
+            alike = beside(*[same[g, :, :] for g in range(4)])
+            return below(mm(alike[0:256, :], block), mm(alike[256:512, :], block))
+
         own_copy(s).wait_recv()
-        ret_copy(s).wait_send()
-        own_copy(s).wait_send()
-        back_sum[...] = returned_sum(t)
         for h in range(2):
             rows = pl.ds(h * 512, 512)
             own_sum[rows, :] = own_buf[s, rows, :].astype(F32) + own_peer[s, rows, :].astype(F32)
             own_lin[rows, :] = mm_t(x[rows, :], n_in_t[s, :, 0:128])
+
+        @pl.when(s < LAYERS - 1)
+        def _():
+            here = picked(x[0:512, :], x[512:1024, :]).astype(BF16)
+            sent_x[...] = here
+            sent_lin[...] = mm_t(here, n_in_t[s, :, 0:128])
+            sent_sum[...] = picked(own_buf[s, 0:512, :], own_buf[s, 512:1024, :]) + picked(
+                own_peer[s, 0:512, :], own_peer[s, 512:1024, :])
+
+        for k in range(4):
+            ret_copy(s, k).wait_recv()
+            relay_copy(s, k).start()
+        ret_copy(s).wait_send()
+        own_copy(s).wait_send()
+        sent_back[...] = returned_sent(t)
+        back_sum[...] = returned_sum(t)
         relay_copy(s).wait_recv()
+
+        @pl.when(s < LAYERS - 1)
+        def _():
+            back = sent_back[...] + returned_sent(1 - t)
+            total = (sent_sum[...] + back).astype(BF16)
+            lin = sent_lin[...] + mm_t(total, n_in_t[s, :, 128:256])
+            hidden = jnp.maximum(lin, 0.0).astype(BF16)
+            update = norm_centred(mm(hidden, n_out_mid[s, :, :]))
+            fill_fwd(s + 1, (sent_x[...].astype(F32) + update).astype(BF16))
+            for k in range(4):
+                fwd_copy(s + 1, k).start()
 
         back = back_sum[...] + returned_sum(1 - t)
         for h in range(2):
@@ -342,12 +388,6 @@
             hidden = jnp.maximum(lin, 0.0).astype(BF16)
             update = norm_centred(mm(hidden, n_out_mid[s, :, :]))
             x[rows, :] = (x[rows, :].astype(F32) + update).astype(BF16)
-
-        @pl.when(s < LAYERS - 1)
-        def _():
-            fill_fwd(s + 1)
-            for k in range(4):
-                fwd_copy(s + 1, k).start()
 
         @pl.when(s < LAYERS - 1)
         def _():
@@ -385,6 +425,7 @@
     dma = pltpu.SemaphoreType.DMA
     packed = (edges // 128, 128)
     scratch = [
+        pltpu.VMEM(packed, I32),
         pltpu.VMEM(packed, I32),
         pltpu.VMEM(packed, I32),
         pltpu.SMEM((1, 1), I32),
@@ -407,6 +448,11 @@
         pltpu.VMEM((512, 256), F32),
         pltpu.VMEM((1024, 128), F32),
         pltpu.VMEM((1024, 128), F32),
+        pltpu.VMEM((4, 512, 128), BF16),
+        pltpu.VMEM((512, 128), BF16),
+        pltpu.VMEM((512, 128), F32),
+        pltpu.VMEM((512, 128), F32),
+        pltpu.VMEM((512, 128), F32),
         pltpu.VMEM((LAYERS, 128, 384), BF16),
         pltpu.VMEM((LAYERS, 128, 256), BF16),
         pltpu.VMEM((LAYERS, 128, 128), BF16),

time: 63.1 us -> 61.9 us (0.981)
  Pallas kernels: 61.6 us -> 60.3 us
    pallas_call x1, Pallas kernels: 60.5 us -> 59.3 us  [local(): pl.pallas_call(functools.partial(kernel, doms, tile), out_shape=(pltpu.VM...]
where the time goes in v7:
time: 61.9 us; the launch traced here: 61.8 us
  Pallas kernels  60.3 us (97%)
  between operations  1.45 us (2%)
    pallas_call x1, Pallas kernels, local(): pl.pallas_call(functools.partial(kernel, doms, tile), out_shape=(pltpu.VM...  59.3 us

profile of v7, /device:TPU:1, one launch (start us, length us, event | category | flops | bytes accessed | tf_op | source)
XLA Modules:
  0.0 61.8 jit_solution(16325331564196058621)
XLA Ops:
  1.3 59.3 %shard_map.113 = (bf16[1024,128]{1,0:T(8,128)(2,1)S(1)}, bf16[4096,128]{1,0:T(8,128)(2,1)S(1)}) custom-call(bf16[1024,128]{1,0:T(8,128)(2,1)} %x_hbm.1, bf16[4096,128]{1,0:T(8,128)(2,1)} %e_hbm.1, s32[32,128]{1,0:T(8,128)} %bitcast.9, s32[32,128]{1,0:T(8,128)} %bitcast.10, s32[1,1]{1,0:T(1,128)} %bitcast.6.cnt_hbm, s32[4,128]{1,0:T(4,128)} %bitcast.11, ...), custom_call_target="tpu_custom_call" | custom-call | tf_op jit(solution)/shard_map/pallas_call | solution.py:473
  60.5 1.1 %shard_map.114 = (bf16[1024,128]{1,0:T(8,128)(2,1)}, bf16[4096,128]{1,0:T(8,128)(2,1)}) custom-call(bf16[1024,128]{1,0:T(8,128)(2,1)S(1)} %get-tuple-element.4.x, bf16[4096,128]{1,0:T(8,128)(2,1)S(1)} %get-tuple-element.5.e), custom_call_target="tpu_custom_call" | custom-call | tf_op jit(solution)/shard_map/pallas_call | solution.py:492

commit v8 on v7

--- a/solution.py
+++ b/solution.py
@@ -141,6 +141,7 @@
     w_o2[...] = jnp.zeros_like(w_o2)
 
     loads[0].wait()
+    loads[1].wait()
     for k in range(4):
         row = sidx[pl.ds(k, 1), :]
         wide = column(row)
@@ -162,7 +163,6 @@
         for k in range(4):
             fwd_buf[layer, k, :, :] = rows[k * 128 : (k + 1) * 128, :]
 
-    loads[1].wait()
     fill_fwd(0, picked(x[0:512, :], x[512:1024, :]).astype(BF16))
     for copy in loads[2:6]:
         copy.wait()

time: 61.9 us -> 61.9 us (level)
  no operation moved by 1% of the time
where the time goes in v8:
time: 61.9 us; the launch traced here: 61.8 us
  Pallas kernels  60.3 us (97%)
  between operations  1.45 us (2%)
    pallas_call x1, Pallas kernels, local(): pl.pallas_call(functools.partial(kernel, doms, tile), out_shape=(pltpu.VM...  59.3 us

profile of v8, /device:TPU:1, one launch (start us, length us, event | category | flops | bytes accessed | tf_op | source)
XLA Modules:
  0.0 61.8 jit_solution(11006333653495189249)
XLA Ops:
  1.3 59.3 %shard_map.113 = (bf16[1024,128]{1,0:T(8,128)(2,1)S(1)}, bf16[4096,128]{1,0:T(8,128)(2,1)S(1)}) custom-call(bf16[1024,128]{1,0:T(8,128)(2,1)} %x_hbm.1, bf16[4096,128]{1,0:T(8,128)(2,1)} %e_hbm.1, s32[32,128]{1,0:T(8,128)} %bitcast.9, s32[32,128]{1,0:T(8,128)} %bitcast.10, s32[1,1]{1,0:T(1,128)} %bitcast.6.cnt_hbm, s32[4,128]{1,0:T(4,128)} %bitcast.11, ...), custom_call_target="tpu_custom_call" | custom-call | tf_op jit(solution)/shard_map/pallas_call | solution.py:473
  60.5 1.1 %shard_map.114 = (bf16[1024,128]{1,0:T(8,128)(2,1)}, bf16[4096,128]{1,0:T(8,128)(2,1)}) custom-call(bf16[1024,128]{1,0:T(8,128)(2,1)S(1)} %get-tuple-element.4.x, bf16[4096,128]{1,0:T(8,128)(2,1)S(1)} %get-tuple-element.5.e), custom_call_target="tpu_custom_call" | custom-call | tf_op jit(solution)/shard_map/pallas_call | solution.py:492
